TPU v7x, 32 devices: a whole 2x2x4 slice. The times are simulated.
32 devices in a mesh: dp: 4 (over x, core), tensor: 8 (over z, y).
Axes of the slice: x: 2, y: 2, z: 4, core: 2. Of those that a mesh axis runs over, the one named last changes fastest.
Arguments:
- activations: bfloat16 [1024, 5120], P('dp'), may hold values from -6 to 6
- grad_out: bfloat16 [1024, 5120], P('dp'), may hold values from -6 to 6
- gate_pre: bfloat16 [1024, 7168], P('dp', 'tensor'), may hold values from -8 to 8
- up_pre: bfloat16 [1024, 7168], P('dp', 'tensor'), may hold values from -6 to 6
- gate_up: bfloat16 [5120, 2, 7168], P('dp', None, 'tensor'), may hold values from -0.078125 to 0.078125
- down_weight: bfloat16 [5120, 7168], P('dp', 'tensor'), may hold values from -0.0625 to 0.0625
Outputs:
- grad_input: bfloat16 [1024, 5120], P('dp')
- grad_gate_up: float32 [5120, 2, 7168], P('dp', None, 'tensor')
- grad_down: float32 [5120, 7168], P('dp', 'tensor')
All inputs are finite; a program needn't handle non-finite values.
Results may differ from a plain program's by a relative error of at most 0.017.
Values may be sent and summed in bfloat16 or wider, within the bound.
A program may use at most 128 MiB of HBM per device.

v0:
```python
import jax
import jax.numpy as jnp
from jax import lax
from jax.experimental import pallas as pl
from jax.experimental.pallas import tpu as pltpu
from jax.sharding import PartitionSpec as P

MESH = pl.DeviceIdType.MESH
ANY = pl.BlockSpec(memory_space=pl.ANY)
VMEM = pl.BlockSpec(memory_space=pltpu.VMEM)


def remote(src, dst, send, recv, device):
    return pltpu.make_async_remote_copy(
        src_ref=src, dst_ref=dst, send_sem=send, recv_sem=recv, device_id=device, device_id_type=MESH
    )


def greet(axes):
    barrier = pltpu.get_barrier_semaphore()
    count = 0
    for axis in axes:
        n = lax.axis_size(axis)
        me = lax.axis_index(axis)
        for s in range(1, n):
            pl.semaphore_signal(
                barrier, inc=1, device_id={axis: lax.rem(me + s, n)}, device_id_type=MESH
            )
        count += n - 1
    pl.semaphore_wait(barrier, count)


def spread(cid, block, wide=()):
    n = lax.axis_size("dp")
    m = lax.axis_size("tensor")
    w = len(wide)
    rows, width = block.shape[1:]

    def kernel(*refs):
        block_ref = refs[0]
        wide_refs = refs[1 : 1 + w]
        out_ref = refs[1 + w]
        wide_outs = refs[2 + w : 2 + 2 * w]
        s1, r1, s2, r2, sw, rw, local = refs[2 + 2 * w :]
        me = lax.axis_index("dp")
        j = lax.axis_index("tensor")
        partner = me + 1 - 2 * lax.rem(me, 2)
        greet(("dp", "tensor"))
        sends = []
        for s in range(1, n):
            p = lax.rem(me + s, n)
            sends.append(
                remote(block_ref.at[p], out_ref.at[me, j], s1.at[s], r1.at[me], {"dp": p})
            )
            sends[-1].start()
        locals_ = [pltpu.make_async_copy(block_ref.at[me], out_ref.at[me, j], local.at[w])]
        locals_[-1].start()
        for a in range(w):
            for s in range(1, n // 2):
                q = lax.rem(me + 2 * s, n)
                sends.append(
                    remote(wide_refs[a], wide_outs[a].at[me], sw.at[a, s], rw.at[a, me], {"dp": q})
                )
                sends[-1].start()
        for a in range(w):
            sends.append(
                remote(wide_refs[a], wide_outs[a].at[me], sw.at[a, 0], rw.at[a, me], {"dp": partner})
            )
            sends[-1].start()
            locals_.append(pltpu.make_async_copy(wide_refs[a], wide_outs[a].at[me], local.at[a]))
            locals_[-1].start()
        for s in range(1, n):
            p = lax.rem(me + n - s, n)
            remote(block_ref.at[p], out_ref.at[p, j], s1.at[s], r1.at[p], {"dp": p}).wait_recv()
        locals_[0].wait()
        lines = m // 2
        row, column = j // 2, lax.rem(j, 2)
        facing = j + 1 - 2 * column
        first, last = row == 0, row == lines - 1

        def hop(kind, r, device):
            k = 2 * r + column
            return remote(
                out_ref.at[:, k], out_ref.at[:, k], s2.at[kind, r], r2.at[k], {"tensor": device}
            )

        def up(r):
            return hop(0, r, lax.rem(j + 2, m))

        def down(r):
            return hop(1, r, lax.rem(j + m - 2, m))

        def across(r):
            return hop(2, r, facing)

        for d in range(lines):
            below, above = row - d, row + d

            @pl.when(below >= 0)
            def _():
                if d > 0:
                    up(below).wait_recv()
                pl.when(jnp.logical_not(last))(lambda: up(below).start())
                if d == 0:
                    pl.when(jnp.logical_not(first))(lambda: down(row).start())
                across(below).start()

            if d > 0:

                @pl.when(above < lines)
                def _():
                    down(above).wait_recv()
                    pl.when(jnp.logical_not(first))(lambda: down(above).start())
                    across(above).start()

        for a in range(w):
            for s in range(1, n // 2):
                q = lax.rem(me + n - 2 * s, n)
                remote(
                    wide_refs[a], wide_outs[a].at[q], sw.at[a, s], rw.at[a, q], {"dp": q}
                ).wait_recv()
                sends.append(
                    remote(
                        wide_outs[a].at[q],
                        wide_outs[a].at[q],
                        sw.at[a, n // 2 + s - 1],
                        rw.at[a, q],
                        {"dp": partner},
                    )
                )
                sends[-1].start()
        for a in range(w):
            locals_[1 + a].wait()
            for s in range(n // 2):
                q = lax.rem(partner + 2 * s, n)
                remote(
                    wide_refs[a], wide_outs[a].at[q], sw.at[a, s], rw.at[a, q], {"dp": partner}
                ).wait_recv()
        for r in range(lines):
            k = 2 * r + 1 - column
            remote(
                out_ref.at[:, k], out_ref.at[:, k], s2.at[2, r], r2.at[k], {"tensor": facing}
            ).wait_recv()
            across(r).wait_send()
            went_up = jnp.logical_and(jnp.logical_not(last), r <= row)
            went_down = jnp.logical_and(jnp.logical_not(first), r >= row)
            pl.when(went_up)(lambda: up(r).wait_send())
            pl.when(went_down)(lambda: down(r).wait_send())
        for copy in sends:
            copy.wait_send()

    dma = pltpu.SemaphoreType.DMA
    shapes = [jax.ShapeDtypeStruct((n, m, rows, width), block.dtype)]
    shapes += [jax.ShapeDtypeStruct((n,) + a.shape, a.dtype) for a in wide]
    return pl.pallas_call(
        kernel,
        out_shape=shapes,
        in_specs=[VMEM] * (1 + w),
        out_specs=[ANY] * (1 + w),
        scratch_shapes=[
            dma((n,)),
            dma((n,)),
            dma((3, m // 2)),
            dma((m,)),
            dma((max(w, 1), n)),
            dma((max(w, 1), n)),
            dma((w + 1,)),
        ],
        compiler_params=pltpu.CompilerParams(collective_id=cid, has_side_effects=True),
    )(block, *wide)


def trade(cid, parts):
    n, m, rows, width = parts.shape

    def kernel(src, dst, send, recv, local):
        j = lax.axis_index("tensor")
        greet(("tensor",))
        sends = []
        for s in range(1, m):
            k = lax.rem(j + s, m)
            sends.append(remote(src.at[:, k], dst.at[j], send.at[s], recv.at[j], {"tensor": k}))
            sends[-1].start()
        own = pltpu.make_async_copy(src.at[:, j], dst.at[j], local)
        own.start()
        for s in range(1, m):
            k = lax.rem(j + m - s, m)
            remote(src.at[:, k], dst.at[k], send.at[s], recv.at[k], {"tensor": k}).wait_recv()
        own.wait()
        for copy in sends:
            copy.wait_send()

    dma = pltpu.SemaphoreType.DMA
    return pl.pallas_call(
        kernel,
        out_shape=jax.ShapeDtypeStruct((m, n, rows, width), parts.dtype),
        in_specs=[ANY],
        out_specs=ANY,
        scratch_shapes=[dma((m,)), dma((m,)), dma],
        compiler_params=pltpu.CompilerParams(collective_id=cid, has_side_effects=True),
    )(parts)


def add_over_dp(partial):
    n = partial.shape[0]
    me = lax.axis_index("dp")
    core = lax.rem(me, 2)
    pairs = partial.reshape((n // 2, 2) + partial.shape[1:])
    other = lax.dynamic_index_in_dim(pairs, 1 - core, 1, keepdims=False).astype(jnp.bfloat16)
    keep = lax.dynamic_index_in_dim(pairs, core, 1, keepdims=False)
    came = lax.ppermute(other, "dp", [(i, i ^ 1) for i in range(n)])
    half = keep + came.astype(jnp.float32)
    mine = me // 2
    total = lax.dynamic_index_in_dim(half, mine, 0, keepdims=False)
    for s in range(1, n // 2):
        piece = lax.dynamic_index_in_dim(half, lax.rem(mine + s, n // 2), 0, keepdims=False)
        came = lax.ppermute(
            piece.astype(jnp.bfloat16), "dp", [(i, (i + 2 * s) % n) for i in range(n)]
        )
        total = total + came.astype(jnp.float32)
    return total.astype(jnp.bfloat16)


def paired_weight(x_cols, grad_gate, grad_up, scale):
    depth, slab = x_cols.shape
    width = grad_gate.shape[1]
    tile = 128 if slab % 128 == 0 else slab

    def kernel(x_ref, gate_ref, up_ref, out_ref):
        for i, ref in enumerate((gate_ref, up_ref)):
            total = lax.dot_general(
                x_ref[...], ref[...], (((0,), (0,)), ((), ())), preferred_element_type=jnp.float32
            )
            out_ref[:, i, :] = total / scale

    whole = pl.BlockSpec((depth, width), lambda i: (0, 0))
    return pl.pallas_call(
        kernel,
        grid=(slab // tile,),
        out_shape=jax.ShapeDtypeStruct((slab, 2, width), jnp.float32),
        in_specs=[pl.BlockSpec((depth, tile), lambda i: (0, i)), whole, whole],
        out_specs=pl.BlockSpec((tile, 2, width), lambda i: (i, 0, 0)),
        cost_estimate=pl.CostEstimate(
            flops=4 * depth * slab * width, bytes_accessed=8 * slab * width, transcendentals=0
        ),
    )(x_cols, grad_gate, grad_up)


def per_device(activations, grad_out, gate_pre, up_pre, gate_up, down_weight):
    tokens, model = activations.shape
    slab, hidden_width = down_weight.shape
    n = lax.axis_size("dp")
    m = lax.axis_size("tensor")
    rows = tokens // m
    j = lax.axis_index("tensor")

    def own_rows(a):
        piece = lax.dynamic_slice_in_dim(a, j * rows, rows, 0)
        return piece.reshape(rows, n, slab).transpose(1, 0, 2)

    dy, gate_all, up_all = spread(1, own_rows(grad_out), (gate_pre, up_pre))
    dy_cols = dy.reshape(n * tokens, slab)
    partial = jnp.dot(dy_cols, down_weight, preferred_element_type=jnp.float32)
    grad_h = add_over_dp(partial.reshape(n, tokens, hidden_width))
    x, grad_h_all = spread(2, own_rows(activations), (grad_h,))
    x_cols = x.reshape(n * tokens, slab)

    def flat(a):
        return a.reshape(n * tokens, hidden_width).astype(jnp.float32)

    gate_wide, up_wide, grad_h = flat(gate_all), flat(up_all), flat(grad_h_all)
    gate_sigmoid = jax.nn.sigmoid(gate_wide)
    gate_silu = gate_wide * gate_sigmoid
    hidden = (gate_silu * up_wide).astype(jnp.bfloat16)
    grad_gate = grad_h * up_wide * gate_sigmoid * (1.0 + gate_wide * (1.0 - gate_sigmoid))
    grad_gate = grad_gate.astype(jnp.bfloat16)
    grad_up = (grad_h * gate_silu).astype(jnp.bfloat16)
    grad_hidden = jnp.concatenate([grad_gate, grad_up], axis=1)

    part = lax.dot_general(
        grad_hidden,
        gate_up.reshape(slab, 2 * hidden_width),
        (((1,), (1,)), ((), ())),
        preferred_element_type=jnp.float32,
    ).astype(jnp.bfloat16)
    parts = trade(3, part.reshape(n, m, rows, slab))
    summed = jnp.sum(parts.astype(jnp.float32), axis=0).astype(jnp.bfloat16)
    (gathered,) = spread(4, summed)
    grad_input = gathered.transpose(1, 2, 0, 3).reshape(tokens, model)

    def weight(a, b):
        total = lax.dot_general(
            a, b, (((0,), (0,)), ((), ())), preferred_element_type=jnp.float32
        )
        return total / n

    grad_gate_up = paired_weight(x_cols, grad_gate, grad_up, float(n))
    grad_down = weight(dy_cols, hidden)
    return (grad_input, grad_gate_up, grad_down)


def solution(mesh):
    in_specs = (
        P("dp", None),
        P("dp", None),
        P("dp", "tensor"),
        P("dp", "tensor"),
        P("dp", None, "tensor"),
        P("dp", "tensor"),
    )
    out_specs = (P("dp", None), P("dp", None, "tensor"), P("dp", "tensor"))
    return jax.shard_map(
        per_device, mesh=mesh, in_specs=in_specs, out_specs=out_specs, check_vma=False
    )
```

profile of v0, /device:TPU:0, one launch (start us, length us, event | category | flops | bytes accessed | tf_op | source)
XLA Modules:
  0.0 263.1 jit_solution(10911394919055683646)
XLA Ops:
  0.6 0.0 copy-start
  0.7 1.3 constant_dynamic-slice_fusion
  1.9 0.7 copy.22
  2.7 49.0 %shard_map.85 = (bf16[4,8,32,1280]{3,2,1,0:T(8,128)(2,1)}, bf16[4,256,896]{2,1,0:T(8,128)(2,1)}, bf16[4,256,896]{2,1,0:T(8,128)(2,1)}) custom-call(bf16[4,32,1280]{2,1,0:T(8,128)(2,1)} %bitcast.85, bf16[256,896]{1,0:T(8,128)(2,1)} %refs_1_.1, bf16[256,896]{1,0:T(8,128)(2,1)} %refs_2_.1), custom_call_target="tpu_custom_call" | custom-call | tf_op jit(solution)/shard_map/pallas_call | solution.py:155
  51.7 0.0 copy-done
  51.7 4.6 %fusion.16 = f32[2,2,256,896]{3,2,1,0:T(8,128)S(1)} fusion(bf16[2,2,256,1280]{3,2,1,0:T(8,128)(2,1)} %bitcast.87, bf16[1280,896]{1,0:T(8,128)(2,1)S(1)} %copy-done), kind=kOutput, calls=%fused_computation.25 | convolution fusion | flops 2348810240 | bytes 8585216 | tf_op jit(solution)/shard_map/dot_general | solution.py:263
  56.3 0.0 copy-start.3
  56.3 1.8 copy-done.3
  58.1 1.0 fusion.18
  59.1 0.0 collective-permute-start
  59.1 0.8 copy.23
  59.9 0.0 copy-start.2
  59.9 5.4 %copy.18 = bf16[160,8,2,896]{3,1,2,0:T(8,128)(2,1)} copy(bf16[160,8,2,896]{3,2,1,0:T(2,128)(2,1)} %bitcast.76) | data formatting | bytes 9175040
  65.3 0.0 copy-done.2
  65.3 0.0 copy-start.4
  65.3 2.7 %fusion.15 = bf16[4,256,896]{2,1,0:T(8,128)(2,1)S(1)} fusion(bf16[4,256,896]{2,1,0:T(8,128)(2,1)S(1)} %copy-done.2, bf16[4,256,896]{2,1,0:T(8,128)(2,1)} %get-tuple-element.10), kind=kLoop, calls=%fused_computation.24 | loop fusion | flops 7340032 | bytes 5505024 | tf_op jit(solution)/shard_map/convert_element_type | solution.py:274
  68.1 0.0 copy-start.7
  68.1 0.0 collective-permute-done
  68.1 0.0 copy-done.4
  68.1 0.2 bitcast_add_fusion
  68.3 0.1 fusion.20
  68.4 0.6 collective-permute-start.1
  69.0 0.8 copy-done.7
  69.8 4.5 %convolution_multiply_fusion = f32[1280,896]{1,0:T(8,128)} fusion(bf16[1024,1280]{1,0:T(8,128)(2,1)S(1)} %bitcast.88, bf16[1024,896]{1,0:T(8,128)(2,1)S(1)} %bitcast.82), kind=kOutput, calls=%fused_computation.2 | convolution fusion | flops 2349957120 | bytes 9043968 | tf_op jit(solution)/shard_map/dot_general | solution.py:292
  74.3 7.0 %collective-permute-done.1 = bf16[256,896]{1,0:T(8,128)(2,1)S(1)} collective-permute-done((bf16[256,896]{1,0:T(8,128)(2,1)S(1)}, bf16[256,896]{1,0:T(8,128)(2,1)S(1)}, u32[]{:S(2)}, u32[]{:S(2)}) %collective-permute-start.1) | collective-permute-done | bytes 458784 | tf_op jit(solution)/shard_map/ppermute | solution.py:217
  81.4 0.9 fusion.19.refs_1_
  82.2 0.0 slice-start
  82.2 45.0 %shard_map.86 = (bf16[4,8,32,1280]{3,2,1,0:T(8,128)(2,1)}, bf16[4,256,896]{2,1,0:T(8,128)(2,1)}) custom-call(bf16[4,32,1280]{2,1,0:T(8,128)(2,1)} %bitcast.83, bf16[256,896]{1,0:T(8,128)(2,1)} %fusion.19.refs_1_), custom_call_target="tpu_custom_call" | custom-call | tf_op jit(solution)/shard_map/pallas_call | solution.py:155
  127.3 0.0 slice-start.1
  127.3 3.6 %fusion.2 = (bf16[1024,896]{1,0:T(8,128)(2,1)S(1)}, bf16[1024,896]{1,0:T(8,128)(2,1)S(1)}) fusion(bf16[4,256,896]{2,1,0:T(8,128)(2,1)S(1)} %copy-done.2, bf16[4,256,896]{2,1,0:T(8,128)(2,1)} %get-tuple-element.9, bf16[4,256,896]{2,1,0:T(8,128)(2,1)} %get-tuple-element.10), kind=kLoop, calls=%fused_computation.6 | loop fusion | flops 14680064 | bytes 9175040 | tf_op jit(solution)/shard_map/convert_element_type | solution.py:276
  130.9 0.0 copy-start.5
  130.9 0.0 copy-start.6
  130.9 0.0 slice-done
  131.0 0.0 slice-done.1
  131.0 6.2 %convolution_convert_fusion = bf16[1024,1280]{1,0:T(8,128)(2,1)} fusion(bf16[1280,1792]{1,0:T(8,128)(2,1)S(1)} %bitcast.79, bf16[1024,896]{1,0:T(8,128)(2,1)S(1)} %get-tuple-element.14.up_ref, bf16[1024,896]{1,0:T(8,128)(2,1)S(1)} %get-tuple-element.13.gate_ref), kind=kOutput, calls=%fused_computation.3 | convolution fusion | flops 4706271232 | bytes 10878976 | tf_op jit(solution)/shard_map/dot_general | solution.py:280
  137.2 0.0 copy-done.5
  137.2 0.0 copy-done.6
  137.2 45.2 %shard_map.87 = bf16[8,4,32,1280]{3,2,1,0:T(8,128)(2,1)} custom-call(bf16[4,8,32,1280]{3,2,1,0:T(8,128)(2,1)} %bitcast.81), custom_call_target="tpu_custom_call" | custom-call | tf_op jit(solution)/shard_map/pallas_call | solution.py:194
  182.4 2.9 %reduce_sum.12.refs_0_ = bf16[4,32,1280]{2,1,0:T(8,128)(2,1)} reduce(bf16[8,4,32,1280]{3,2,1,0:T(8,128)(2,1)} %shard_map.87, bf16[]{:T(256)} %constant.51.clone.1), dimensions={0}, to_apply=%region_0.1 | reduce | flops 1146880 | bytes 2949122 | tf_op jit(solution)/shard_map/reduce_sum | solution.py:287
  185.3 58.9 %shard_map.88 = bf16[4,8,32,1280]{3,2,1,0:T(8,128)(2,1)} custom-call(bf16[4,32,1280]{2,1,0:T(8,128)(2,1)} %reduce_sum.12.refs_0_), custom_call_target="tpu_custom_call" | custom-call | tf_op jit(solution)/shard_map/pallas_call | solution.py:155
  244.3 3.8 %copy.13 = bf16[8,32,4,1280]{3,2,1,0:T(4,128)(2,1)S(1)} copy(bf16[8,32,4,1280]{3,1,0,2:T(8,128)(2,1)} %bitcast.74) | data formatting | bytes 5242880 | tf_op jit(solution)/shard_map/transpose | solution.py:289
  248.0 2.0 copy.19
  250.0 0.0 copy-start.1
  250.0 13.1 %shard_map.89 = f32[1280,2,896]{2,1,0:T(2,128)} custom-call(bf16[1024,1280]{1,0:T(8,128)(2,1)} %bitcast.89, bf16[1024,896]{1,0:T(8,128)(2,1)} %copy-done.5, bf16[1024,896]{1,0:T(8,128)(2,1)} %copy-done.6), custom_call_target="tpu_custom_call" | custom-call | flops 4697620480 | bytes 9175040 | tf_op jit(solution)/shard_map/pallas_call | solution.py:237
  263.1 0.0 copy-done.1
  (1 shorter events, 0.0 us)
Async XLA Ops:
  0.6 51.0 %copy-start = (bf16[1280,896]{1,0:T(8,128)(2,1)S(1)}, bf16[1280,896]{1,0:T(8,128)(2,1)}, u32[]{:S(2)}) copy-start(bf16[1280,896]{1,0:T(8,128)(2,1)} %param.11) | copy-start | bytes 6881284
  56.3 1.8 copy-start.3
  59.1 9.0 %collective-permute-start = (bf16[2,256,896]{2,1,0:T(8,128)(2,1)}, bf16[2,256,896]{2,1,0:T(8,128)(2,1)S(1)}, u32[]{:S(2)}, u32[]{:S(2)}) collective-permute-start(bf16[2,256,896]{2,1,0:T(8,128)(2,1)} %fusion.18), channel_id=1, source_target_pairs={{0,8},{8,0},{16,24},{24,16},{1,9},{9,1},{17,25},{25,17},{2,10},{10... | collective-permute-start | bytes 2752520 | tf_op jit(solution)/shard_map/ppermute | solution.py:211
  59.9 5.4 %copy-start.2 = (bf16[4,256,896]{2,1,0:T(8,128)(2,1)S(1)}, bf16[4,256,896]{2,1,0:T(8,128)(2,1)}, u32[]{:S(2)}) copy-start(bf16[4,256,896]{2,1,0:T(8,128)(2,1)} %get-tuple-element.11) | copy-start | bytes 5505028
  65.3 2.8 %copy-start.4 = (f32[2,2,256,896]{3,2,1,0:T(8,128)S(1)}, f32[2,2,256,896]{3,2,1,0:T(8,128)}, u32[]{:S(2)}) copy-start(f32[2,2,256,896]{3,2,1,0:T(8,128)} %copy-done.3) | copy-start | bytes 11010052
  68.1 1.7 copy-start.7
  68.4 13.0 %collective-permute-start.1 = (bf16[256,896]{1,0:T(8,128)(2,1)S(1)}, bf16[256,896]{1,0:T(8,128)(2,1)S(1)}, u32[]{:S(2)}, u32[]{:S(2)}) collective-permute-start(bf16[256,896]{1,0:T(8,128)(2,1)S(1)} %fusion.20), channel_id=1, source_target_pairs={{0,16},{8,24},{16,0},{24,8},{1,17},{9,25},{17,1},{25,9},{2,18},{10... | collective-permute-start | bytes 1376264 | tf_op jit(solution)/shard_map/ppermute | solution.py:217
  82.2 48.7 %slice-start = ((s8[4587520]{0:T(1024)(128)(4,1)}), s8[393216]{0:T(1024)(128)(4,1)S(1)}, s32[]{:S(2)}) async-start(s8[4587520]{0:T(1024)(128)(4,1)} %bitcast.77), calls=%async_computation | async-start | bytes 786432
  127.3 3.7 %slice-start.1 = ((s8[4587520]{0:T(1024)(128)(4,1)}), s8[4194304]{0:T(1024)(128)(4,1)S(1)}, s32[]{:S(2)}) async-start(s8[4587520]{0:T(1024)(128)(4,1)} %bitcast.77), calls=%async_computation.1 | async-start | bytes 8388608
  130.9 6.3 %copy-start.5 = (bf16[1024,896]{1,0:T(8,128)(2,1)}, bf16[1024,896]{1,0:T(8,128)(2,1)S(1)}, u32[]{:S(2)}) copy-start(bf16[1024,896]{1,0:T(8,128)(2,1)S(1)} %get-tuple-element.13.gate_ref) | copy-start | bytes 5505028
  130.9 6.3 %copy-start.6 = (bf16[1024,896]{1,0:T(8,128)(2,1)}, bf16[1024,896]{1,0:T(8,128)(2,1)S(1)}, u32[]{:S(2)}) copy-start(bf16[1024,896]{1,0:T(8,128)(2,1)S(1)} %get-tuple-element.14.up_ref) | copy-start | bytes 5505028
  250.0 13.1 %copy-start.1 = (bf16[1280,896]{1,0:T(8,128)(2,1)S(1)}, bf16[1280,896]{1,0:T(8,128)(2,1)}, u32[]{:S(2)}) copy-start(bf16[1280,896]{1,0:T(8,128)(2,1)} %param.11) | copy-start | bytes 6881284
where the time goes:
time: 264 us; the launch traced here: 263 us
  Pallas kernels  211 us (80%)
  local copies, waits for them, and re-layouts  17.7 us (7%)
  matrix products  15.3 us (6%)
  other arithmetic  10.4 us (4%)
  waiting for transfers between devices  7.05 us (3%)
    pallas_call x3, Pallas kernels, spread(): pl.pallas_call(kernel, out_shape=shapes, in_specs=[VMEM] * (1 + w), out_s...  153 us
    pallas_call x1, Pallas kernels, trade(): pl.pallas_call(kernel, out_shape=jax.ShapeDtypeStruct((m, n, rows, width)...  45.2 us
    pallas_call x1, Pallas kernels, paired_weight(): pl.pallas_call(kernel, grid=(slab // tile,), out_shape=jax.ShapeDtypeStru...  13.1 us
    unnamed x22, local copies, waits for them, and re-layouts  10.1 us
    ppermute x1, waiting for transfers between devices, add_over_dp(): lax.ppermute(piece.astype(jnp.bfloat16), 'dp', [(i, (i + 2 * s) % n) for...  7.05 us
    dot_general x1, matrix products, per_device(): lax.dot_general(grad_hidden, gate_up.reshape(slab, 2 * hidden_width), (((...  6.22 us
  transfers between devices with their start and end apart: 2, of which 1 were waited for; matrix products, arithmetic and copies ran while one was open for 5% of the time, Pallas kernels for 0%

commit v1 on v0

v1 whole, which is shorter than its diff:
```python
import jax
import jax.numpy as jnp
from jax import lax
from jax.experimental import pallas as pl
from jax.experimental.pallas import tpu as pltpu
from jax.sharding import PartitionSpec as P

MESH = pl.DeviceIdType.MESH
ANY = pl.BlockSpec(memory_space=pl.ANY)
VMEM = pl.BlockSpec(memory_space=pltpu.VMEM)
F32 = jnp.float32
BF16 = jnp.bfloat16


def remote(src, dst, send, recv, device):
    return pltpu.make_async_remote_copy(
        src_ref=src, dst_ref=dst, send_sem=send, recv_sem=recv, device_id=device, device_id_type=MESH
    )


def tile_of(size):
    for tile in (256, 128):
        if size % tile == 0:
            return tile
    return size


class Line:
    def __init__(self, block, send, recv, j, m):
        self.block, self.send, self.recv = block, send, recv
        self.m, self.lines = m, m // 2
        self.row, self.column = j // 2, lax.rem(j, 2)
        self.facing = j + 1 - 2 * self.column
        self.above_me, self.below_me = lax.rem(j + 2, m), lax.rem(j + m - 2, m)
        self.first, self.last = self.row == 0, self.row == self.lines - 1

    def hop(self, kind, r, device):
        k = 2 * r + self.column
        block = self.block(k)
        return remote(block, block, self.send.at[kind, r], self.recv.at[k], {"tensor": device})

    def up(self, r):
        return self.hop(0, r, self.above_me)

    def down(self, r):
        return self.hop(1, r, self.below_me)

    def across(self, r):
        return self.hop(2, r, self.facing)

    def step(self, d):
        below, above = self.row - d, self.row + d

        @pl.when(below >= 0)
        def _():
            if d > 0:
                self.up(below).wait_recv()
            pl.when(jnp.logical_not(self.last))(lambda: self.up(below).start())
            if d == 0:
                pl.when(jnp.logical_not(self.first))(lambda: self.down(self.row).start())
            self.across(below).start()

        if d > 0:

            @pl.when(above < self.lines)
            def _():
                self.down(above).wait_recv()
                pl.when(jnp.logical_not(self.first))(lambda: self.down(above).start())
                self.across(above).start()

    def finish(self):
        for r in range(self.lines):
            k = 2 * r + 1 - self.column
            block = self.block(k)
            remote(
                block, block, self.send.at[2, r], self.recv.at[k], {"tensor": self.facing}
            ).wait_recv()

    def drain(self):
        for r in range(self.lines):
            self.across(r).wait_send()
            went_up = jnp.logical_and(jnp.logical_not(self.last), r <= self.row)
            went_down = jnp.logical_and(jnp.logical_not(self.first), r >= self.row)
            pl.when(went_up)(lambda: self.up(r).wait_send())
            pl.when(went_down)(lambda: self.down(r).wait_send())


def layer(cid, activations, grad_out, gate_pre, up_pre, gate_w, up_w, down_w):
    tokens, model = activations.shape
    slab, width = down_w.shape
    n = lax.axis_size("dp")
    m = lax.axis_size("tensor")
    chips, lines = n // 2, m // 2
    rows = tokens // m
    aligned = slab % 128 == 0
    if not aligned:
        activations, grad_out = (
            a.reshape(tokens, n, slab).transpose(1, 0, 2) for a in (activations, grad_out)
        )
    tile = tile_of(slab)
    tiles = slab // tile
    lot = 16

    def kernel(
        x_in, dy_in, gate_in, up_in, w0_in, w1_in, down_in,
        out, wg0, wg1, wd,
        dy, x, gate, up, grad_h, down, w0, w1,
        keep, swap, pair, came, part, beside, carry, rising, falling, mine, final,
        wbuf,
        line_s, line_r, hop_s, hop_r, ge_s, ge_r, pair_s, pair_r, ex_s, ex_r, g_s, g_r,
        y_s, y_r, z_s, up_r, dn_r, load, store,
    ):
        me = lax.axis_index("dp")
        j = lax.axis_index("tensor")
        core = lax.rem(me, 2)
        chip = me // 2
        partner = me + 1 - 2 * core
        z, y = j // 2, lax.rem(j, 2)
        facing = j + 1 - 2 * y
        above, below = lax.rem(j + 2, m), lax.rem(j + m - 2, m)
        first, last = z == 0, z == lines - 1

        def shifted(s):
            return lax.rem(chip + s, chips)

        barrier = pltpu.get_barrier_semaphore()

        def signal(device):
            pl.semaphore_signal(barrier, inc=1, device_id=device, device_id_type=MESH)

        for s in range(1, n):
            signal({"dp": lax.rem(me + s, n)})
        signal({"tensor": facing})
        pl.when(jnp.logical_not(first))(lambda: signal({"tensor": below}))
        pl.when(jnp.logical_not(last))(lambda: signal({"tensor": above}))
        pl.semaphore_wait(barrier, n + (z > 0).astype(jnp.int32) + (z < lines - 1).astype(jnp.int32))

        def own_rows(ref, p):
            r = pl.ds(pl.multiple_of(j * rows, rows), rows)
            if aligned:
                return ref.at[r, pl.ds(pl.multiple_of(p * slab, 128), slab)]
            return ref.at[p, r]

        def own_all(ref, p):
            if aligned:
                return ref.at[:, pl.ds(pl.multiple_of(p * slab, 128), slab)]
            return ref.at[p]

        def block(buf, p, k):
            return buf.at[p, pl.ds(pl.multiple_of(k * rows, rows), rows)]

        def pair_block(buf, c, k):
            return buf.at[pl.ds(2 * c, 2), pl.ds(pl.multiple_of(k * rows, rows), rows)]

        local_loads = [
            pltpu.make_async_copy(src, dst, load.at[i])
            for i, (src, dst) in enumerate(
                ((down_in, down), (w0_in, w0), (w1_in, w1), (gate_in, gate.at[me]), (up_in, up.at[me]))
            )
        ]

        def hop_copy(b, src, buf, p):
            return remote(own_rows(src, p), block(buf, me, j), hop_s.at[b, p], hop_r.at[b, me], {"dp": p})

        def hop_whole(b, src, buf):
            return remote(
                own_all(src, partner), buf.at[me], hop_s.at[b, partner], hop_r.at[b, me], {"dp": partner}
            )

        def hop_own(b, src, buf):
            return pltpu.make_async_copy(own_all(src, me), buf.at[me], hop_s.at[b, me])

        def hop_start(b, src, buf):
            for s in range(1, chips):
                for c in range(2):
                    hop_copy(b, src, buf, 2 * shifted(s) + c).start()
            hop_whole(b, src, buf).start()
            hop_own(b, src, buf).start()

        def hop_arrive(b, buf):
            for s in range(1, chips):
                for c in range(2):
                    q = 2 * shifted(s) + c
                    spot = block(buf, q, j)
                    remote(spot, spot, hop_s.at[b, q], hop_r.at[b, q], {"dp": q}).wait_recv()

        def hop_near(b, src, buf):
            hop_own(b, src, buf).wait()
            spot = buf.at[partner]
            remote(spot, spot, hop_s.at[b, partner], hop_r.at[b, partner], {"dp": partner}).wait_recv()

        def hop_drain(b, src, buf):
            for s in range(1, chips):
                for c in range(2):
                    hop_copy(b, src, buf, 2 * shifted(s) + c).wait_send()
            hop_whole(b, src, buf).wait_send()

        def wide_copy(a, src, buf, s):
            q = partner if s == 0 else 2 * shifted(s) + core
            return remote(src, buf.at[me], ge_s.at[a, s], ge_r.at[a, me], {"dp": q})

        def wide_forward(a, buf, s):
            q = 2 * shifted(s) + core
            return remote(buf.at[q], buf.at[q], ge_s.at[a, chips + s], ge_r.at[a, q], {"dp": partner})

        def wide_wait(a, buf, q):
            remote(buf.at[q], buf.at[q], ge_s.at[a, 0], ge_r.at[a, q], {"dp": q}).wait_recv()

        local_loads[0].start()
        hop_start(0, dy_in, dy)
        for s in range(1, chips):
            wide_copy(0, gate_in, gate, s).start()
        hop_start(1, x_in, x)
        for s in range(1, chips):
            wide_copy(1, up_in, up, s).start()
        wide_copy(0, gate_in, gate, 0).start()
        wide_copy(1, up_in, up, 0).start()
        for copy in local_loads[1:]:
            copy.start()

        def lines_of(buf, base, shifts):
            made = []
            for i, s in enumerate(shifts):
                c = shifted(s)
                made.append(
                    Line(
                        lambda k, c=c: pair_block(buf, c, k),
                        line_s.at[base + i],
                        line_r.at[base + i],
                        j,
                        m,
                    )
                )
            return made

        others = list(range(1, chips))
        dy_lines = lines_of(dy, 0, others)
        x_lines = lines_of(x, chips - 1, others)
        out_lines = lines_of(out, 2 * chips - 2, others + [0])

        def all_of(made, name, *args):
            for line in made:
                getattr(line, name)(*args)

        def multiply(c):
            got = 2 * c + 1 - core
            swap[c] = jnp.dot(dy[got], down[...], preferred_element_type=F32).astype(BF16)
            pair_copy(c).start()
            keep[c] = jnp.dot(dy[2 * c + core], down[...], preferred_element_type=F32)

        def pair_copy(c):
            return remote(swap.at[c], pair.at[c], pair_s.at[c], pair_r.at[c], {"dp": partner})

        def ex_copy(c, s):
            q = 2 * shifted(s) + core
            return remote(swap.at[c], came.at[chip, c], ex_s.at[c, s], ex_r.at[c, chip], {"dp": q})

        def chip_sum(c):
            pair_copy(c).wait()

            @pl.loop(0, tokens // lot)
            def _(i):
                r = pl.ds(i * lot, lot)
                total = keep[c, r] + pair[c, r].astype(F32)
                keep[c, r] = total
                swap[c, r] = total.astype(BF16)

            for s in others:
                ex_copy(c, s).start()

        def g_copy(c):
            spot = grad_h.at[2 * c + core]
            return remote(spot, spot, g_s.at[c], g_r.at[c], {"dp": partner})

        def grad_h_sum(c):
            for s in others:
                q = shifted(s)
                spot = came.at[q, c]
                remote(spot, spot, ex_s.at[c, s], ex_r.at[c, q], {"dp": 2 * q + core}).wait_recv()

            @pl.loop(0, tokens // lot)
            def _(i):
                r = pl.ds(i * lot, lot)
                total = keep[c, r]
                for s in others:
                    total = total + came[shifted(s), c, r].astype(F32)
                grad_h[2 * c + core, r] = total.astype(BF16)

            g_copy(c).start()

        def gates(p):
            @pl.loop(0, tokens // lot)
            def _(i):
                r = pl.ds(i * lot, lot)
                v = gate[p, r].astype(F32)
                u = up[p, r].astype(F32)
                g = grad_h[p, r].astype(F32)
                s = jax.nn.sigmoid(v)
                silu = v * s
                grad_h[p, r] = (silu * u).astype(BF16)
                gate[p, r] = (g * u * s * (1.0 + v * (1.0 - s))).astype(BF16)
                up[p, r] = (g * silu).astype(BF16)

        def input_part(c):
            across = (((1,), (1,)), ((), ()))
            left0 = gate[pl.ds(2 * c, 2)].reshape(2 * tokens, width)
            left1 = up[pl.ds(2 * c, 2)].reshape(2 * tokens, width)
            for i in range(tiles):
                cols = pl.ds(i * tile, tile)
                total = lax.dot_general(left0, w0[cols], across, preferred_element_type=F32)
                total = total + lax.dot_general(left1, w1[cols], across, preferred_element_type=F32)
                part[c, :, :, cols] = total.astype(BF16).reshape(2, tokens, tile)

        def target(i):
            return jnp.where(z < lines // 2, lines - 1 - i, i)

        def y_copy(c, i):
            t = target(i)
            k = 2 * t + 1 - y
            src = part.at[c, :, pl.ds(pl.multiple_of(k * rows, rows), rows)]
            return remote(src, beside.at[c, t], y_s.at[c, t], y_r.at[c, t], {"tensor": facing})

        def climb(c, t):
            return remote(carry.at[c, t], rising.at[c, t], z_s.at[c, t], up_r.at[c, t], {"tensor": above})

        def descend(c, t):
            return remote(carry.at[c, t], falling.at[c, t], z_s.at[c, t], dn_r.at[c, t], {"tensor": below})

        def add_rows(fn):
            for g in range(2):
                for i in range(rows // lot):
                    fn(g, slice(i * lot, (i + 1) * lot), i * lot)

        def item(c, i):
            t = target(i)
            y_copy(c, i).wait_recv()
            rise = jnp.logical_and(t > z, z > 0)
            fall = jnp.logical_and(t < z, z < lines - 1)
            pl.when(rise)(lambda: climb(c, t).wait_recv())
            pl.when(fall)(lambda: descend(c, t).wait_recv())

            def start_of(g, r0):
                r = pl.ds(pl.multiple_of((2 * t + y) * rows + r0, lot), lot)
                return part[c, g, r].astype(F32)

            def plain(g, r, r0):
                carry[c, t, g, r] = (start_of(g, r0) + beside[c, t, g, r].astype(F32)).astype(BF16)

            def risen(g, r, r0):
                total = start_of(g, r0) + beside[c, t, g, r].astype(F32)
                carry[c, t, g, r] = (total + rising[c, t, g, r].astype(F32)).astype(BF16)

            def fallen(g, r, r0):
                total = start_of(g, r0) + beside[c, t, g, r].astype(F32)
                carry[c, t, g, r] = (total + falling[c, t, g, r].astype(F32)).astype(BF16)

            def own(g, r, r0):
                mine[c, g, r] = start_of(g, r0) + beside[c, t, g, r].astype(F32)

            pl.when(rise)(lambda: add_rows(risen))
            pl.when(fall)(lambda: add_rows(fallen))
            edge = jnp.logical_or(
                jnp.logical_and(first, t > z), jnp.logical_and(last, t < z)
            )
            pl.when(edge)(lambda: add_rows(plain))
            pl.when(t == z)(lambda: add_rows(own))
            pl.when(t > z)(lambda: climb(c, t).start())
            pl.when(t < z)(lambda: descend(c, t).start())

        def total_of(c):
            pl.when(z > 0)(lambda: climb(c, z).wait_recv())
            pl.when(z < lines - 1)(lambda: descend(c, z).wait_recv())

            def close(parts):
                def fn(g, r, r0):
                    total = mine[c, g, r]
                    for ref in parts:
                        total = total + ref[c, z, g, r].astype(F32)
                    final[c, g, r] = total.astype(BF16)

                return fn

            pl.when(first)(lambda: add_rows(close((falling,))))
            pl.when(last)(lambda: add_rows(close((rising,))))
            inner = jnp.logical_not(jnp.logical_or(first, last))
            pl.when(inner)(lambda: add_rows(close((rising, falling))))

        def out_copy(c, g):
            p = 2 * c + g
            return remote(final.at[c, g], block(out, me, j), hop_s.at[2, p], hop_r.at[2, me], {"dp": p})

        def out_send(s):
            c = shifted(s)
            if s > 0:
                for g in range(2):
                    out_copy(c, g).start()
            else:
                out_copy(c, 1 - core).start()
                pltpu.make_async_copy(final.at[c, core], block(out, me, j), hop_s.at[2, me]).start()

        def out_arrive(s):
            c = shifted(s)
            if s > 0:
                for g in range(2):
                    q = 2 * c + g
                    spot = block(out, q, j)
                    remote(spot, spot, hop_s.at[2, q], hop_r.at[2, q], {"dp": q}).wait_recv()
            else:
                spot = block(out, partner, j)
                remote(
                    spot, spot, hop_s.at[2, partner], hop_r.at[2, partner], {"dp": partner}
                ).wait_recv()
                pltpu.make_async_copy(final.at[c, core], block(out, me, j), hop_s.at[2, me]).wait()

        def out_drain(s):
            c = shifted(s)
            for g in range(2):
                if s > 0:
                    out_copy(c, g).wait_send()
            if s == 0:
                out_copy(c, 1 - core).wait_send()

        def stored(i):
            rows_i = pl.ds(i * tile, tile)
            return [
                pltpu.make_async_copy(wbuf.at[a, rows_i], ref.at[rows_i], store.at[a, i])
                for a, ref in enumerate((wg0, wg1, wd))
            ]

        def weights(i):
            down_cols = (((0,), (0,)), ((), ()))
            cols = pl.ds(i * tile, tile)
            left = x[:, :, cols].reshape(n * tokens, tile)
            back = dy[:, :, cols].reshape(n * tokens, tile)
            for a, (lhs, ref) in enumerate(((left, gate), (left, up), (back, grad_h))):
                total = lax.dot_general(
                    lhs, ref[...].reshape(n * tokens, width), down_cols, preferred_element_type=F32
                )
                wbuf[a, cols] = (total * (1.0 / n)).astype(BF16)
            for copy in stored(i):
                copy.start()

        hop_arrive(0, dy)
        all_of(dy_lines, "step", 0)
        hop_near(0, dy_in, dy)
        local_loads[0].wait()
        multiply(chip)
        if lines > 1:
            all_of(dy_lines, "step", 1)
        chip_sum(chip)
        for d in range(2, lines):
            all_of(dy_lines, "step", d)
        hop_arrive(1, x)
        all_of(x_lines, "step", 0)
        all_of(dy_lines, "finish")
        for s in others:
            multiply(shifted(s))
        for s in others:
            chip_sum(shifted(s))
        for d in range(1, lines):
            all_of(x_lines, "step", d)
        for s in others:
            q = 2 * shifted(s) + core
            wide_wait(0, gate, q)
            wide_forward(0, gate, s).start()
        for s in others:
            q = 2 * shifted(s) + core
            wide_wait(1, up, q)
            wide_forward(1, up, s).start()
        local_loads[1].wait()
        local_loads[2].wait()
        for s in others + [0]:
            c = shifted(s)
            grad_h_sum(c)
            if s == 0:
                local_loads[3].wait()
                local_loads[4].wait()
            else:
                wide_forward(0, gate, s).wait_send()
                wide_forward(1, up, s).wait_send()
            wide_wait(0, gate, 2 * c + 1 - core)
            wide_wait(1, up, 2 * c + 1 - core)
            g_copy(c).wait_send()
            gates(2 * c + core)
            spot = grad_h.at[2 * c + 1 - core]
            remote(spot, spot, g_s.at[c], g_r.at[c], {"dp": partner}).wait_recv()
            gates(2 * c + 1 - core)
            input_part(c)
            for i in range(lines):
                y_copy(c, i).start()
        all_of(x_lines, "finish")
        hop_near(1, x_in, x)

        spare = list(range(tiles))

        def some(count):
            for _ in range(count):
                if spare:
                    weights(spare.pop(0))

        for s in others:
            for i in range(lines):
                item(shifted(s), i)
            total_of(shifted(s))
            out_send(s)
        some(1)
        half = lines // 2
        for i in range(half):
            item(chip, i)
        for s in others:
            out_arrive(s)
        all_of(out_lines[:-1], "step", 0)
        for i in range(half, lines):
            item(chip, i)
        some(1)
        total_of(chip)
        out_send(0)
        if lines > 1:
            all_of(out_lines[:-1], "step", 1)
        out_arrive(0)
        out_lines[-1].step(0)
        some(1)
        for d in range(2, lines + 1):
            if d < lines:
                all_of(out_lines[:-1], "step", d)
            if d - 1 < lines and d > 1:
                out_lines[-1].step(d - 1)
            some(1)
        some(tiles)
        all_of(out_lines, "finish")

        all_of(dy_lines + x_lines + out_lines, "drain")
        hop_drain(0, dy_in, dy)
        hop_drain(1, x_in, x)
        for s in range(chips):
            wide_copy(0, gate_in, gate, s).wait_send()
            wide_copy(1, up_in, up, s).wait_send()
            for u in others:
                ex_copy(shifted(s), u).wait_send()
            for i in range(lines):
                y_copy(shifted(s), i).wait_send()
                t = target(i)
                pl.when(t > z)(lambda: climb(shifted(s), t).wait_send())
                pl.when(t < z)(lambda: descend(shifted(s), t).wait_send())
            out_drain(s)
        for i in range(tiles):
            for copy in stored(i):
                copy.wait()

    dma = pltpu.SemaphoreType.DMA
    vm = pltpu.VMEM
    flops = 2 * n * tokens * slab * width * 6
    return pl.pallas_call(
        kernel,
        out_shape=[jax.ShapeDtypeStruct((n, tokens, slab), BF16)]
        + [jax.ShapeDtypeStruct((slab, width), BF16)] * 3,
        in_specs=[ANY] * 7,
        out_specs=[VMEM] + [ANY] * 3,
        scratch_shapes=[
            vm((n, tokens, slab), BF16),
            vm((n, tokens, slab), BF16),
            vm((n, tokens, width), BF16),
            vm((n, tokens, width), BF16),
            vm((n, tokens, width), BF16),
            vm((slab, width), BF16),
            vm((slab, width), BF16),
            vm((slab, width), BF16),
            vm((chips, tokens, width), F32),
            vm((chips, tokens, width), BF16),
            vm((chips, tokens, width), BF16),
            vm((chips, chips, tokens, width), BF16),
            vm((chips, 2, tokens, slab), BF16),
            vm((chips, lines, 2, rows, slab), BF16),
            vm((chips, lines, 2, rows, slab), BF16),
            vm((chips, lines, 2, rows, slab), BF16),
            vm((chips, lines, 2, rows, slab), BF16),
            vm((chips, 2, rows, slab), F32),
            vm((chips, 2, rows, slab), BF16),
            vm((3, slab, width), BF16),
            dma((3 * chips - 2, 3, lines)),
            dma((3 * chips - 2, m)),
            dma((3, n)),
            dma((3, n)),
            dma((2, 2 * chips)),
            dma((2, n)),
            dma((chips,)),
            dma((chips,)),
            dma((chips, chips)),
            dma((chips, chips)),
            dma((chips,)),
            dma((chips,)),
            dma((chips, lines)),
            dma((chips, lines)),
            dma((chips, lines)),
            dma((chips, lines)),
            dma((chips, lines)),
            dma((5,)),
            dma((3, tiles)),
        ],
        cost_estimate=pl.CostEstimate(flops=flops, bytes_accessed=40 * slab * width, transcendentals=0),
        compiler_params=pltpu.CompilerParams(
            collective_id=cid, has_side_effects=True, vmem_limit_bytes=66_000_000
        ),
    )(activations, grad_out, gate_pre, up_pre, gate_w, up_w, down_w)


def per_device(activations, grad_out, gate_pre, up_pre, gate_up, down_weight):
    tokens, model = activations.shape
    gathered, grad_gate, grad_up, grad_down = layer(
        1, activations, grad_out, gate_pre, up_pre, gate_up[:, 0, :], gate_up[:, 1, :], down_weight
    )
    grad_input = gathered.transpose(1, 0, 2).reshape(tokens, model)
    grad_gate_up = jnp.stack([grad_gate, grad_up], axis=1).astype(F32)
    return (grad_input, grad_gate_up, grad_down.astype(F32))


def solution(mesh):
    in_specs = (
        P("dp", None),
        P("dp", None),
        P("dp", "tensor"),
        P("dp", "tensor"),
        P("dp", None, "tensor"),
        P("dp", "tensor"),
    )
    out_specs = (P("dp", None), P("dp", None, "tensor"), P("dp", "tensor"))
    return jax.shard_map(
        per_device, mesh=mesh, in_specs=in_specs, out_specs=out_specs, check_vma=False
    )
```

time: 264 us -> 161 us (0.61)
  Pallas kernels: 211 us -> 121 us
  local copies, waits for them, and re-layouts: 17.7 us -> 33.3 us
  matrix products: 15.3 us -> 0 us
  waiting for transfers between devices: 7.05 us -> 0 us
  other arithmetic: 10.4 us -> 5.37 us
    pallas_call x5 -> x1, Pallas kernels: 211 us -> 121 us  [layer(): pl.pallas_call(kernel, out_shape=[jax.ShapeDtypeStruct((n, tokens, slab),...]
    dot_general x3 -> x0, matrix products: 15.3 us -> none  [the longest x1 6.22 us: per_device(): lax.dot_general(grad_hidden, gate_up.reshape(slab, 2 * hidden_width), (((...]
    slice x0 -> x1, local copies, waits for them, and re-layouts: none -> 9.74 us  [per_device(): gate_up[:, 1, :]]
    unnamed x22 -> x4, local copies, waits for them, and re-layouts: 10.1 us -> 17.7 us
    ppermute x2 -> x0, waiting for transfers between devices: 7.05 us -> none  [the longest x1 7.05 us: add_over_dp(): lax.ppermute(piece.astype(jnp.bfloat16), 'dp', [(i, (i + 2 * s) % n) for...]
    reduce_sum x1 -> x0, other arithmetic: 2.92 us -> none  [per_device(): summed = jnp.sum(parts.astype(jnp.float32), axis=0).astype(jnp.bfloat16)]
    squeeze x0 -> x1, local copies, waits for them, and re-layouts: none -> 2.89 us  [per_device(): gate_up[:, 1, :]]
    convert_element_type x3 -> x2, other arithmetic: 7.23 us -> 5.37 us  [the longest x1 2.93 us: per_device(): grad_gate_up = jnp.stack([grad_gate, grad_up], axis=1).astype(F32)]
  transfers between devices with their start and end apart: 2 -> 0, of which waited for: 1 -> 0; matrix products, arithmetic and copies ran while one was open for 5% -> 0% of each run, Pallas kernels for 0% -> 0%
where the time goes in v1:
time: 161 us; the launch traced here: 160 us
  Pallas kernels  121 us (75%)
  local copies, waits for them, and re-layouts  33.3 us (21%)
  other arithmetic  5.37 us (3%)
    pallas_call x1, Pallas kernels, layer(): pl.pallas_call(kernel, out_shape=[jax.ShapeDtypeStruct((n, tokens, slab),...  121 us
    unnamed x4, local copies, waits for them, and re-layouts  17.7 us
    slice x1, local copies, waits for them, and re-layouts, per_device(): gate_up[:, 1, :]  9.74 us

profile of v1, /device:TPU:0, one launch (start us, length us, event | category | flops | bytes accessed | tf_op | source)
XLA Modules:
  0.0 159.9 jit_solution(15944736912556797282)
XLA Ops:
  0.6 9.7 %fusion = (bf16[1280,1,896]{2,1,0:T(2,128)(2,1)S(1)}, bf16[1280,1,896]{2,1,0:T(2,128)(2,1)S(1)}) fusion(bf16[1280,2,896]{2,1,0:T(2,128)(2,1)} %param.10), kind=kLoop, calls=%fused_computation.3 | loop fusion | bytes 9175040 | tf_op jit(solution)/shard_map/slice | solution.py:610
  10.4 2.9 %copy_bitcast_fusion = (bf16[1280,896]{1,0:T(8,128)(2,1)}, bf16[1280,896]{1,0:T(8,128)(2,1)}) fusion(bf16[1280,1,896]{2,1,0:T(2,128)(2,1)S(1)} %get-tuple-element.17, bf16[1280,1,896]{2,1,0:T(2,128)(2,1)S(1)} %get-tuple-element.18), kind=kLoop, calls=%fused_computation.1 | loop fusion | bytes 9175040 | tf_op jit(solution)/shard_map/squeeze | solution.py:610
  13.3 120.5 %shard_map.85 = (bf16[4,256,1280]{2,1,0:T(8,128)(2,1)}, bf16[1280,896]{1,0:T(8,128)(2,1)}, bf16[1280,896]{1,0:T(8,128)(2,1)}, bf16[1280,896]{1,0:T(8,128)(2,1)}) custom-call(bf16[256,5120]{1,0:T(8,128)(2,1)} %x_in.1, bf16[256,5120]{1,0:T(8,128)(2,1)} %dy_in.1, bf16[256,896]{1,0:T(8,128)(2,1)} %gate_in.1, bf16[256,896]{1,0:T(8,128)(2,1)} %up_in.1, ...), custom_call_target="tpu_custom_call" | custom-call | flops 14092861440 | bytes 45875200 | tf_op jit(solution)/shard_map/pallas_call | solution.py:553
  133.8 3.0 %copy.14 = bf16[256,4,1280]{0,2,1:T(8,128)(2,1)S(1)} copy(bf16[256,4,1280]{2,0,1:T(8,128)(2,1)} %bitcast.9) | data formatting | bytes 5242880 | tf_op jit(solution)/shard_map/transpose | solution.py:612
  136.8 2.8 %copy.15 = bf16[256,5120]{1,0:T(8,128)(2,1)} copy(bf16[256,5120]{0,1:T(8,128)(2,1)S(1)} %bitcast.8) | data formatting | bytes 5242880
  139.6 2.9 %maximum_convert_fusion = f32[1280,2,896]{2,0,1:T(8,128)S(1)} fusion(bf16[1280,1,896]{2,0,1:T(8,128)(2,1)} %bitcast.11, bf16[1280,1,896]{2,0,1:T(8,128)(2,1)} %bitcast.10), kind=kLoop, calls=%fused_computation | loop fusion | flops 4587520 | bytes 13762560 | tf_op jit(solution)/shard_map/convert_element_type | solution.py:613
  142.5 0.0 copy-start
  142.5 15.0 %copy.16 = f32[1280,2,896]{2,1,0:T(2,128)} copy(f32[1280,2,896]{2,0,1:T(8,128)S(1)} %maximum_convert_fusion) | data formatting | bytes 18350080
  157.5 0.0 copy-done
  157.5 2.4 %convert_element_type.7 = f32[1280,896]{1,0:T(8,128)} convert(bf16[1280,896]{1,0:T(8,128)(2,1)S(1)} %copy-done) | non-fusion elementwise | flops 1146880 | bytes 6881280 | tf_op jit(solution)/shard_map/convert_element_type | solution.py:614
Async XLA Ops:
  142.5 15.0 %copy-start = (bf16[1280,896]{1,0:T(8,128)(2,1)S(1)}, bf16[1280,896]{1,0:T(8,128)(2,1)}, u32[]{:S(2)}) copy-start(bf16[1280,896]{1,0:T(8,128)(2,1)} %get-tuple-element.10) | copy-start | bytes 6881284

commit v2 on v1

v2 whole, which is shorter than its diff:
```python
import math

import jax
import jax.numpy as jnp
from jax import lax
from jax.experimental import pallas as pl
from jax.experimental.pallas import tpu as pltpu
from jax.sharding import PartitionSpec as P

MESH = pl.DeviceIdType.MESH
ANY = pl.BlockSpec(memory_space=pl.ANY)
F32 = jnp.float32
BF16 = jnp.bfloat16


def remote(src, dst, send, recv, device):
    return pltpu.make_async_remote_copy(
        src_ref=src, dst_ref=dst, send_sem=send, recv_sem=recv, device_id=device, device_id_type=MESH
    )


SCOPED = False


class Plain:
    def __enter__(self):
        return self

    def __exit__(self, *args):
        return None


def scope(name):
    return jax.named_scope(name) if SCOPED else Plain()


def tile_of(size):
    for tile in (256, 128):
        if size % tile == 0:
            return tile
    return size


class Line:
    def __init__(self, block, send, recv, j, m):
        self.block, self.send, self.recv = block, send, recv
        self.m, self.lines = m, m // 2
        self.row, self.column = j // 2, lax.rem(j, 2)
        self.facing = j + 1 - 2 * self.column
        self.above_me, self.below_me = lax.rem(j + 2, m), lax.rem(j + m - 2, m)
        self.first, self.last = self.row == 0, self.row == self.lines - 1

    def hop(self, kind, r, device):
        k = 2 * r + self.column
        block = self.block(k)
        return remote(block, block, self.send.at[kind, r], self.recv.at[k], {"tensor": device})

    def up(self, r):
        return self.hop(0, r, self.above_me)

    def down(self, r):
        return self.hop(1, r, self.below_me)

    def across(self, r):
        return self.hop(2, r, self.facing)

    def sideways(self):
        self.across(self.row).start()

    def lengthways(self):
        pl.when(jnp.logical_not(self.last))(lambda: self.up(self.row).start())
        pl.when(jnp.logical_not(self.first))(lambda: self.down(self.row).start())

    def step(self, d):
        if d == 0:
            self.lengthways()
            self.sideways()
            return
        below, above = self.row - d, self.row + d

        @pl.when(below >= 0)
        def _():
            self.up(below).wait_recv()
            pl.when(jnp.logical_not(self.last))(lambda: self.up(below).start())
            self.across(below).start()

        @pl.when(above < self.lines)
        def _():
            self.down(above).wait_recv()
            pl.when(jnp.logical_not(self.first))(lambda: self.down(above).start())
            self.across(above).start()

    def finish(self):
        for r in range(self.lines):
            k = 2 * r + 1 - self.column
            block = self.block(k)
            remote(
                block, block, self.send.at[2, r], self.recv.at[k], {"tensor": self.facing}
            ).wait_recv()

    def drain(self):
        for r in range(self.lines):
            self.across(r).wait_send()
            went_up = jnp.logical_and(jnp.logical_not(self.last), r <= self.row)
            went_down = jnp.logical_and(jnp.logical_not(self.first), r >= self.row)
            pl.when(went_up)(lambda: self.up(r).wait_send())
            pl.when(went_down)(lambda: self.down(r).wait_send())


def layer(cid, activations, grad_out, gate_pre, up_pre, gate_up, down_w):
    tokens, model = activations.shape
    slab, width = down_w.shape
    n = lax.axis_size("dp")
    m = lax.axis_size("tensor")
    chips, lines = n // 2, m // 2
    rows = tokens // m
    aligned = slab % 128 == 0
    if not aligned:
        activations, grad_out = (
            a.reshape(tokens, n, slab).transpose(1, 0, 2) for a in (activations, grad_out)
        )
    raw = width % 128 == 0
    mixed = (gate_up,) if raw else (gate_up[:, 0, :], gate_up[:, 1, :])
    tile = tile_of(slab)
    tiles = slab // tile
    lot = 16
    half = tokens // 2

    def kernel(*refs):
        single(refs[: len(mixed)], *refs[len(mixed) :])

    def single(
        mixed_in, x_in, dy_in, gate_in, up_in, down_in,
        out, wg0, wg1, wd,
        dy, x, gate, up, grad_h, down, both, w0, w1, gathered,
        keep, swap, pair, came, part, beside, carry, rising, falling, mine, final,
        wbuf,
        line_s, line_r, hop_s, hop_r, ge_s, ge_r, gx_s, gx_r, gf_s, gf_r, xs_s, xs_r,
        pair_s, pair_r, ex_s, ex_r, g_s, g_r,
        y_s, y_r, z_s, up_r, dn_r, load, store, leave,
    ):
        me = lax.axis_index("dp")
        j = lax.axis_index("tensor")
        core = lax.rem(me, 2)
        chip = me // 2
        partner = me + 1 - 2 * core
        z, y = j // 2, lax.rem(j, 2)
        facing = j + 1 - 2 * y
        above, below = lax.rem(j + 2, m), lax.rem(j + m - 2, m)
        first, last = z == 0, z == lines - 1
        others = list(range(1, chips))

        def shifted(s):
            return lax.rem(chip + s, chips)

        barrier = pltpu.get_barrier_semaphore()

        def signal(device):
            pl.semaphore_signal(barrier, inc=1, device_id=device, device_id_type=MESH)

        for s in range(1, n):
            signal({"dp": lax.rem(me + s, n)})
        signal({"tensor": facing})
        pl.when(jnp.logical_not(first))(lambda: signal({"tensor": below}))
        pl.when(jnp.logical_not(last))(lambda: signal({"tensor": above}))
        pl.semaphore_wait(barrier, n + (z > 0).astype(jnp.int32) + (z < lines - 1).astype(jnp.int32))

        my_half = pl.ds(pl.multiple_of(core * half, half), half)
        its_half = pl.ds(pl.multiple_of((1 - core) * half, half), half)
        my_rows = pl.ds(pl.multiple_of(j * rows, rows), rows)

        def cols_of(ref, r, p):
            if aligned:
                return ref.at[r, pl.ds(pl.multiple_of(p * slab, 128), slab)]
            return ref.at[p, r]

        def block(buf, p, k):
            return buf.at[p, pl.ds(pl.multiple_of(k * rows, rows), rows)]

        local_loads = [
            pltpu.make_async_copy(src, dst, load.at[i])
            for i, (src, dst) in enumerate(((down_in, down), (gate_in, gate.at[me]), (up_in, up.at[me])))
        ]
        weight_loads = [
            pltpu.make_async_copy(src, dst, load.at[3 + i])
            for i, (src, dst) in enumerate(
                ((mixed_in[0], both),) if raw else zip(mixed_in, (w0, w1))
            )
        ]

        def take_apart():
            for copy in weight_loads:
                copy.wait()
            if raw:

                @pl.loop(0, slab // lot)
                def _(i):
                    r = pl.ds(i * lot, lot)
                    flat = both[r].reshape(lot, 2 * width)
                    w0[r] = flat[:, :width]
                    w1[r] = flat[:, width:]

        def hop_copy(p):
            return remote(
                cols_of(dy_in, my_rows, p), block(dy, me, j), hop_s.at[0, p], hop_r.at[0, me], {"dp": p}
            )

        def near_copy(b, src, buf):
            return remote(
                cols_of(src, slice(None), partner),
                buf.at[me],
                hop_s.at[b, partner],
                hop_r.at[b, me],
                {"dp": partner},
            )

        def own_copy(b, src, buf):
            return pltpu.make_async_copy(cols_of(src, slice(None), me), buf.at[me], hop_s.at[b, me])

        def near_wait(b, src, buf):
            own_copy(b, src, buf).wait()
            spot = buf.at[partner]
            remote(spot, spot, hop_s.at[b, partner], hop_r.at[b, partner], {"dp": partner}).wait_recv()

        def x_copy(s, g, h):
            p = 2 * shifted(s) + g
            r = pl.ds(h * half, half)
            return remote(
                cols_of(x_in, r, p), x.at[me, r], xs_s.at[p, h], xs_r.at[me, h], {"dp": p}
            )

        def x_wait():
            near_wait(1, x_in, x)
            for s in others:
                for g in range(2):
                    for h in range(2):
                        q = 2 * shifted(s) + g
                        spot = x.at[q, pl.ds(h * half, half)]
                        remote(spot, spot, xs_s.at[q, h], xs_r.at[q, h], {"dp": q}).wait_recv()

        wide = ((gate_in, gate), (up_in, up))

        def wide_near(a):
            src, buf = wide[a]
            return remote(src, buf.at[me], ge_s.at[a], ge_r.at[a], {"dp": partner})

        def wide_near_wait(a):
            local_loads[1 + a].wait()
            spot = wide[a][1].at[partner]
            remote(spot, spot, ge_s.at[a], ge_r.at[a], {"dp": partner}).wait_recv()

        def wide_far(a, g, s):
            p = 2 * chip + g
            spot = wide[a][1].at[p, my_half]
            return remote(spot, spot, gx_s.at[a, g, s], gx_r.at[a, p], {"dp": 2 * shifted(s) + core})

        def wide_forward(a, p):
            spot = wide[a][1].at[p, my_half]
            return remote(spot, spot, gf_s.at[a, p], gf_r.at[a, p], {"dp": partner})

        def wide_far_wait(a, p):
            spot = wide[a][1].at[p, my_half]
            remote(spot, spot, gf_s.at[a, p], gx_r.at[a, p], {"dp": partner}).wait_recv()

        def wide_forward_wait(a, p):
            spot = wide[a][1].at[p, its_half]
            remote(spot, spot, gf_s.at[a, p], gf_r.at[a, p], {"dp": partner}).wait_recv()

        def lines_of(buf, base, shifts):
            made = []
            for g in range(2):
                for s in shifts:
                    i = base + len(made)
                    q = 2 * shifted(s) + g
                    made.append(
                        Line(lambda k, q=q: block(buf, q, k), line_s.at[i], line_r.at[i], j, m)
                    )
            return made

        dy_lines = lines_of(dy, 0, others)
        far_lines = lines_of(gathered, 2 * chips - 2, others)
        near_lines = lines_of(gathered, 4 * chips - 4, [0])

        def all_of(made, name, *args):
            for line in made:
                getattr(line, name)(*args)

        def pair_copy(p):
            return remote(swap.at[p], pair.at[p], pair_s.at[p], pair_r.at[p], {"dp": partner})

        def multiply(p):
            swap[p] = jnp.dot(dy[p, its_half], down[...], preferred_element_type=F32).astype(BF16)
            pair_copy(p).start()
            keep[p] = jnp.dot(dy[p, my_half], down[...], preferred_element_type=F32)

        def ex_copy(p, s):
            q = 2 * shifted(s) + core
            return remote(swap.at[p], came.at[chip, p], ex_s.at[p, s], ex_r.at[p, chip], {"dp": q})

        def chip_sum(p):
            pair_copy(p).wait()

            @pl.loop(0, half // lot)
            def _(i):
                r = pl.ds(i * lot, lot)
                total = keep[p, r] + pair[p, r].astype(F32)
                keep[p, r] = total
                swap[p, r] = total.astype(BF16)

            for s in others:
                ex_copy(p, s).start()

        def g_copy(p):
            spot = grad_h.at[p, my_half]
            return remote(spot, spot, g_s.at[p], g_r.at[p], {"dp": partner})

        def g_wait(p):
            spot = grad_h.at[p, its_half]
            remote(spot, spot, g_s.at[p], g_r.at[p], {"dp": partner}).wait_recv()

        def grad_h_sum(p):
            for s in others:
                q = shifted(s)
                spot = came.at[q, p]
                remote(spot, spot, ex_s.at[p, s], ex_r.at[p, q], {"dp": 2 * q + core}).wait_recv()

            @pl.loop(0, half // lot)
            def _(i):
                r = pl.ds(i * lot, lot)
                total = keep[p, r]
                for s in others:
                    total = total + came[shifted(s), p, r].astype(F32)
                grad_h[p, pl.ds(pl.multiple_of(core * half + i * lot, lot), lot)] = total.astype(BF16)

            g_copy(p).start()

        def gates(p):
            @pl.loop(0, tokens // lot)
            def _(i):
                r = pl.ds(i * lot, lot)
                v = gate[p, r].astype(F32)
                u = up[p, r].astype(F32)
                g = grad_h[p, r].astype(F32)
                s = jax.nn.sigmoid(v)
                silu = v * s
                grad_h[p, r] = (silu * u).astype(BF16)
                gate[p, r] = (g * u * s * (1.0 + v * (1.0 - s))).astype(BF16)
                up[p, r] = (g * silu).astype(BF16)

        def input_part(p):
            across = (((1,), (1,)), ((), ()))
            for i in range(tiles):
                cols = pl.ds(i * tile, tile)
                total = lax.dot_general(gate[p], w0[cols], across, preferred_element_type=F32)
                total = total + lax.dot_general(up[p], w1[cols], across, preferred_element_type=F32)
                part[p, :, cols] = total.astype(BF16)

        orders = [sorted(range(lines), key=lambda t: (-abs(t - r), t)) for r in range(lines)]

        def target(i):
            t = jnp.int32(0)
            for r in range(lines):
                t = jnp.where(z == r, orders[r][i], t)
            return t

        def y_copy(p, i):
            t = target(i)
            src = block(part, p, 2 * t + 1 - y)
            return remote(src, beside.at[p, t], y_s.at[p, t], y_r.at[p, t], {"tensor": facing})

        def climb(p, t):
            return remote(carry.at[p, t], rising.at[p, t], z_s.at[p, t], up_r.at[p, t], {"tensor": above})

        def descend(p, t):
            return remote(carry.at[p, t], falling.at[p, t], z_s.at[p, t], dn_r.at[p, t], {"tensor": below})

        def add_rows(fn):
            for i in range(rows // lot):
                fn(slice(i * lot, (i + 1) * lot), i * lot)

        def item(p, i):
            t = target(i)
            y_copy(p, i).wait_recv()
            rise = jnp.logical_and(t > z, z > 0)
            fall = jnp.logical_and(t < z, z < lines - 1)
            pl.when(rise)(lambda: climb(p, t).wait_recv())
            pl.when(fall)(lambda: descend(p, t).wait_recv())

            def start_of(r, r0):
                q = pl.ds(pl.multiple_of((2 * t + y) * rows + r0, lot), lot)
                return part[p, q].astype(F32) + beside[p, t, r].astype(F32)

            def plain(r, r0):
                carry[p, t, r] = start_of(r, r0).astype(BF16)

            def risen(r, r0):
                carry[p, t, r] = (start_of(r, r0) + rising[p, t, r].astype(F32)).astype(BF16)

            def fallen(r, r0):
                carry[p, t, r] = (start_of(r, r0) + falling[p, t, r].astype(F32)).astype(BF16)

            def own(r, r0):
                mine[p, r] = start_of(r, r0)

            pl.when(rise)(lambda: add_rows(risen))
            pl.when(fall)(lambda: add_rows(fallen))
            edge = jnp.logical_or(jnp.logical_and(first, t > z), jnp.logical_and(last, t < z))
            pl.when(edge)(lambda: add_rows(plain))
            pl.when(t == z)(lambda: add_rows(own))
            pl.when(t > z)(lambda: climb(p, t).start())
            pl.when(t < z)(lambda: descend(p, t).start())

        def total_of(p):
            pl.when(z > 0)(lambda: climb(p, z).wait_recv())
            pl.when(z < lines - 1)(lambda: descend(p, z).wait_recv())

            def close(parts):
                def fn(r, r0):
                    total = mine[p, r]
                    for ref in parts:
                        total = total + ref[p, z, r].astype(F32)
                    final[p, r] = total.astype(BF16)

                return fn

            pl.when(first)(lambda: add_rows(close((falling,))))
            pl.when(last)(lambda: add_rows(close((rising,))))
            inner = jnp.logical_not(jnp.logical_or(first, last))
            pl.when(inner)(lambda: add_rows(close((rising, falling))))

        def out_copy(p):
            return remote(final.at[p], block(gathered, me, j), hop_s.at[2, p], hop_r.at[2, me], {"dp": p})

        def out_local():
            return pltpu.make_async_copy(final.at[me], block(gathered, me, j), hop_s.at[2, me])

        def out_wait(q):
            spot = block(gathered, q, j)
            remote(spot, spot, hop_s.at[2, q], hop_r.at[2, q], {"dp": q}).wait_recv()

        grads = ((x, gate, wg0), (x, up, wg1), (dy, grad_h, wd))

        def stored(a, i):
            r = pl.ds(i * tile, tile)
            return pltpu.make_async_copy(wbuf.at[a, r], grads[a][2].at[r], store.at[a, i])

        def weights(a, i):
            over_rows = (((0,), (0,)), ((), ()))
            cols = pl.ds(i * tile, tile)
            left, right, _ = grads[a]
            total = lax.dot_general(
                left[:, :, cols].reshape(n * tokens, tile),
                right[...].reshape(n * tokens, width),
                over_rows,
                preferred_element_type=F32,
            )
            wbuf[a, cols] = (total * (1.0 / n)).astype(BF16)
            stored(a, i).start()

        local_loads[0].start()
        for s in others:
            for g in range(2):
                hop_copy(2 * shifted(s) + g).start()
        near_copy(0, dy_in, dy).start()
        own_copy(0, dy_in, dy).start()
        for a in range(2):
            wide_near(a).start()
            local_loads[1 + a].start()

        def send_wide(g):
            for a in range(2):
                for s in others:
                    wide_far(a, g, s).start()

        def afar(g):
            return [2 * shifted(s) + g for s in others]

        def chunk(p, far, tag):
            with scope("gsum" + tag):
                grad_h_sum(p)
            with scope("gwait" + tag):
                for a in range(2):
                    if far:
                        wide_forward(a, p).wait_send()
                        wide_forward_wait(a, p)
                    else:
                        for s in others:
                            wide_far(a, 1 if far is None else 0, s).wait_send()
                g_copy(p).wait_send()
                g_wait(p)
            with scope("gates" + tag):
                gates(p)
            with scope("part" + tag):
                input_part(p)
                for i in range(lines):
                    y_copy(p, i).start()

        def far_forward(g):
            with scope("fwd%d" % g):
                for p in afar(g):
                    for a in range(2):
                        wide_far_wait(a, p)
                        wide_forward(a, p).start()

        def far_chunk(g):
            for p in afar(g):
                chunk(p, True, "B%d" % g)

        def near_chunk(g):
            chunk(2 * chip + g, None if g else False, "A%d" % g)

        def items(ps, tag, which):
            for p in ps:
                for i in which:
                    with scope("item" + tag + str(i)):
                        item(p, i)

        def far_total(g):
            with scope("totalB%d" % g):
                for p in afar(g):
                    total_of(p)
                    out_copy(p).start()

        def near_total(g):
            with scope("totalA%d" % g):
                total_of(2 * chip + g)
                pl.when(core == g)(lambda: out_local().start())
                pl.when(core != g)(lambda: out_copy(partner).start())

        def send_x(g, h):
            for s in others:
                x_copy(s, g, h).start()

        spare = [(2, i) for i in range(tiles)]

        def some(count):
            for _ in range(count):
                if spare:
                    a, i = spare.pop(0)
                    with scope("w%d%d" % (a, i)):
                        weights(a, i)

        every = range(lines)
        with scope("wide"):
            wide_near_wait(0)
            wide_near_wait(1)
            send_wide(0)
        with scope("near"):
            near_wait(0, dy_in, dy)
            local_loads[0].wait()
        with scope("mul0"):
            multiply(2 * chip)
        with scope("dyhop"):
            for g in range(2):
                for q in afar(g):
                    spot = block(dy, q, j)
                    remote(spot, spot, hop_s.at[0, q], hop_r.at[0, q], {"dp": q}).wait_recv()
                all_of(dy_lines[g * (chips - 1) : (g + 1) * (chips - 1)], "step", 0)
        with scope("sum0"):
            chip_sum(2 * chip)
            send_wide(1)
            multiply(2 * chip + 1)
        if lines > 1:
            with scope("dy1"):
                all_of(dy_lines, "step", 1)
        with scope("sum0b"):
            chip_sum(2 * chip + 1)
        for copy in weight_loads:
            copy.start()
        near_copy(1, x_in, x).start()
        own_copy(1, x_in, x).start()
        for d in range(2, lines):
            with scope("dy%d" % d):
                all_of(dy_lines, "step", d)
            if d == 2:
                with scope("apart"):
                    take_apart()
        if lines <= 2:
            take_apart()
        for g in range(2):
            with scope("dyfin"):
                all_of(dy_lines[g * (chips - 1) : (g + 1) * (chips - 1)], "finish")
            with scope("mul1"):
                for p in afar(g):
                    multiply(p)
        with scope("sum1"):
            for g in range(2):
                for p in afar(g):
                    chip_sum(p)
        mid = lines // 2
        far_forward(0)
        far_chunk(0)
        items(afar(0), "B0", range(1))
        far_forward(1)
        far_chunk(1)
        items(afar(0), "B0", range(1, lines))
        near_chunk(0)
        send_x(0, 0)
        items(afar(1), "B1", range(1))
        near_chunk(1)
        far_total(0)
        items(afar(1), "B1", range(1, lines))
        items([2 * chip], "A0", range(mid))
        far_total(1)
        for g, h in ((0, 1), (1, 0), (1, 1)):
            send_x(g, h)
        items([2 * chip], "A0", range(mid, lines))
        some(1)
        items([2 * chip + 1], "A1", range(1))
        with scope("outB0"):
            for g in range(2):
                for q in afar(g):
                    out_wait(q)
            all_of(far_lines, "sideways")
        items([2 * chip + 1], "A1", range(1, lines))
        all_of(far_lines, "lengthways")
        near_total(0)
        some(1)
        near_total(1)
        if lines > 1:
            with scope("outB1"):
                all_of(far_lines, "step", 1)
        with scope("outA0"):
            out_wait(partner)
            out_local().wait()
            all_of(near_lines, "step", 0)
        for d in range(2, lines + 1):
            if d < lines:
                with scope("outB%d" % d):
                    all_of(far_lines, "step", d)
            some(2)
            if d == lines - 1:
                some(tiles)
                with scope("xwait"):
                    x_wait()
                spare += [(a, i) for i in range(tiles) for a in range(2)]
                some(1)
            with scope("outA%d" % (d - 1)):
                all_of(near_lines, "step", d - 1)
            some(2)
        some(2 * tiles)

        def leaving(q):
            return pltpu.make_async_copy(gathered.at[q], out.at[q], leave.at[q])

        for made, shifts in ((far_lines, others), (near_lines, [0])):
            with scope("outfin"):
                for i, line in enumerate(made):
                    line.finish()
                    leaving(2 * shifted(shifts[i % len(shifts)]) + i // len(shifts)).start()

        with scope("drain"):
            all_of(dy_lines + far_lines + near_lines, "drain")
            for g in range(2):
                for p in afar(g):
                    hop_copy(p).wait_send()
                    out_copy(p).wait_send()
                for s in others:
                    for h in range(2):
                        x_copy(s, g, h).wait_send()
            near_copy(0, dy_in, dy).wait_send()
            near_copy(1, x_in, x).wait_send()
            out_copy(partner).wait_send()
            for a in range(2):
                wide_near(a).wait_send()
            for s in range(chips):
                for g in range(2):
                    p = 2 * shifted(s) + g
                    for u in others:
                        ex_copy(p, u).wait_send()
                    for i in every:
                        y_copy(p, i).wait_send()
                        t = target(i)
                        pl.when(t > z)(lambda: climb(p, t).wait_send())
                        pl.when(t < z)(lambda: descend(p, t).wait_send())
        with scope("stores"):
            for q in range(n):
                leaving(q).wait()
            for a in range(3):
                for i in range(tiles):
                    stored(a, i).wait()

    dma = pltpu.SemaphoreType.DMA
    vm = pltpu.VMEM
    flops = 2 * n * tokens * slab * width * 6
    return pl.pallas_call(
        kernel,
        out_shape=[jax.ShapeDtypeStruct((n, tokens, slab), BF16)]
        + [jax.ShapeDtypeStruct((slab, width), BF16)] * 3,
        in_specs=[ANY] * (5 + len(mixed)),
        out_specs=[ANY] * 4,
        scratch_shapes=[
            vm((n, tokens, slab), BF16),
            vm((n, tokens, slab), BF16),
            vm((n, tokens, width), BF16),
            vm((n, tokens, width), BF16),
            vm((n, tokens, width), BF16),
            vm((slab, width), BF16),
            vm((slab, 2, width) if raw else (16, 128), BF16),
            vm((slab, width), BF16),
            vm((slab, width), BF16),
            vm((n, tokens, slab), BF16),
            vm((n, half, width), F32),
            vm((n, half, width), BF16),
            vm((n, half, width), BF16),
            vm((chips, n, half, width), BF16),
            vm((n, tokens, slab), BF16),
            vm((n, lines, rows, slab), BF16),
            vm((n, lines, rows, slab), BF16),
            vm((n, lines, rows, slab), BF16),
            vm((n, lines, rows, slab), BF16),
            vm((n, rows, slab), F32),
            vm((n, rows, slab), BF16),
            vm((3, slab, width), BF16),
            dma((4 * chips - 2, 3, lines)),
            dma((4 * chips - 2, m)),
            dma((3, n)),
            dma((3, n)),
            dma((2,)),
            dma((2,)),
            dma((2, 2, chips)),
            dma((2, n)),
            dma((2, n)),
            dma((2, n)),
            dma((n, 2)),
            dma((n, 2)),
            dma((n,)),
            dma((n,)),
            dma((n, chips)),
            dma((n, chips)),
            dma((n,)),
            dma((n,)),
            dma((n, lines)),
            dma((n, lines)),
            dma((n, lines)),
            dma((n, lines)),
            dma((n, lines)),
            dma((5,)),
            dma((3, tiles)),
            dma((n,)),
        ],
        cost_estimate=pl.CostEstimate(flops=flops, bytes_accessed=40 * slab * width, transcendentals=0),
        compiler_params=pltpu.CompilerParams(
            collective_id=cid, has_side_effects=True, vmem_limit_bytes=66_000_000
        ),
    )(*mixed, activations, grad_out, gate_pre, up_pre, down_w)


def spread_out(gathered, grad_gate, grad_up, grad_down):
    n, tokens, slab = gathered.shape
    width = grad_down.shape[1]
    steps = min(math.gcd(tokens // 16, slab // 16), 4)
    t, r = tokens // steps, slab // steps

    def kernel(all_ref, gate_ref, up_ref, down_ref, input_ref, pair_ref, last_ref):
        for q in range(n):
            input_ref[:, q * slab : (q + 1) * slab] = all_ref[q]
        pair_ref[:, 0, :] = gate_ref[...].astype(F32)
        pair_ref[:, 1, :] = up_ref[...].astype(F32)
        last_ref[...] = down_ref[...].astype(F32)

    flat = pl.BlockSpec((r, width), lambda i: (i, 0))
    return pl.pallas_call(
        kernel,
        grid=(steps,),
        out_shape=[
            jax.ShapeDtypeStruct((tokens, n * slab), BF16),
            jax.ShapeDtypeStruct((slab, 2, width), F32),
            jax.ShapeDtypeStruct((slab, width), F32),
        ],
        in_specs=[pl.BlockSpec((n, t, slab), lambda i: (0, i, 0)), flat, flat, flat],
        out_specs=[
            pl.BlockSpec((t, n * slab), lambda i: (i, 0)),
            pl.BlockSpec((r, 2, width), lambda i: (i, 0, 0)),
            flat,
        ],
        cost_estimate=pl.CostEstimate(
            flops=slab * width, bytes_accessed=18 * slab * width, transcendentals=0
        ),
    )(gathered, grad_gate, grad_up, grad_down)


def per_device(activations, grad_out, gate_pre, up_pre, gate_up, down_weight):
    made = layer(1, activations, grad_out, gate_pre, up_pre, gate_up, down_weight)
    return tuple(spread_out(*made))


def solution(mesh):
    in_specs = (
        P("dp", None),
        P("dp", None),
        P("dp", "tensor"),
        P("dp", "tensor"),
        P("dp", None, "tensor"),
        P("dp", "tensor"),
    )
    out_specs = (P("dp", None), P("dp", None, "tensor"), P("dp", "tensor"))
    return jax.shard_map(
        per_device, mesh=mesh, in_specs=in_specs, out_specs=out_specs, check_vma=False
    )
```

time: 161 us -> 118 us (0.73)
  local copies, waits for them, and re-layouts: 33.3 us -> 0 us
  other arithmetic: 5.37 us -> 0 us
  Pallas kernels: 121 us -> 117 us
    unnamed x4 -> x0, local copies, waits for them, and re-layouts: 17.7 us -> none
    pallas_call x1, Pallas kernels: 121 us -> 106 us  [layer(): pl.pallas_call(kernel, out_shape=[jax.ShapeDtypeStruct((n, tokens, slab),...]
    pallas_call x0 -> x1, Pallas kernels: none -> 10.5 us  [spread_out(): pl.pallas_call(kernel, grid=(steps,), out_shape=[jax.ShapeDtypeStruct((to...]
    slice x1 -> x0, local copies, waits for them, and re-layouts: 9.74 us -> none  [per_device(): gate_up[:, 1, :]]
    convert_element_type x2 -> x0, other arithmetic: 5.37 us -> none  [the longest x1 2.93 us: per_device(): grad_gate_up = jnp.stack([grad_gate, grad_up], axis=1).astype(F32)]
    transpose x1 -> x0, local copies, waits for them, and re-layouts: 2.97 us -> none  [per_device(): grad_input = gathered.transpose(1, 0, 2).reshape(tokens, model)]
    squeeze x1 -> x0, local copies, waits for them, and re-layouts: 2.89 us -> none  [per_device(): gate_up[:, 1, :]]
where the time goes in v2:
time: 118 us; the launch traced here: 117 us
  Pallas kernels  117 us (99%)
    pallas_call x1, Pallas kernels, layer(): pl.pallas_call(kernel, out_shape=[jax.ShapeDtypeStruct((n, tokens, slab),...  106 us
    pallas_call x1, Pallas kernels, spread_out(): pl.pallas_call(kernel, grid=(steps,), out_shape=[jax.ShapeDtypeStruct((to...  10.5 us

profile of v2, /device:TPU:0, one launch (start us, length us, event | category | flops | bytes accessed | tf_op | source)
XLA Modules:
  0.0 117.3 jit_solution(2211590470296313722)
XLA Ops:
  0.6 106.2 %shard_map.85 = (bf16[4,256,1280]{2,1,0:T(8,128)(2,1)}, bf16[1280,896]{1,0:T(8,128)(2,1)}, bf16[1280,896]{1,0:T(8,128)(2,1)}, bf16[1280,896]{1,0:T(8,128)(2,1)}) custom-call(bf16[1280,2,896]{2,1,0:T(2,128)(2,1)} %refs_0_.1, bf16[256,5120]{1,0:T(8,128)(2,1)} %refs_1_.1, bf16[256,5120]{1,0:T(8,128)(2,1)} %refs_2_.1, bf16[256,896]{1,0:T(8,128)(2,1)} %refs_3_.1, ...), custom_call_target="tpu_custom_call" | custom-call | flops 14092861440 | bytes 45875200 | tf_op jit(solution)/shard_map/pallas_call | solution.py:686
  106.9 10.5 %shard_map.86 = (bf16[256,5120]{1,0:T(8,128)(2,1)}, f32[1280,2,896]{2,1,0:T(2,128)}, f32[1280,896]{1,0:T(8,128)}) custom-call(bf16[4,256,1280]{2,1,0:T(8,128)(2,1)} %get-tuple-element.7.all_ref, bf16[1280,896]{1,0:T(8,128)(2,1)} %get-tuple-element.8.gate_ref, bf16[1280,896]{1,0:T(8,128)(2,1)} %get-tuple-element.9.up_ref, ...), custom_call_target="tpu_custom_call" | custom-call | flops 1146880 | bytes 20643840 | tf_op jit(solution)/shard_map/pallas_call | solution.py:763

commit v3 on v2

--- a/solution.py
+++ b/solution.py
@@ -41,28 +41,38 @@
     return size
 
 
+def pick(z, values):
+    chosen = jnp.int32(0)
+    for r, value in enumerate(values):
+        chosen = jnp.where(z == r, value, chosen)
+    return chosen
+
+
 class Line:
-    def __init__(self, block, send, recv, j, m):
-        self.block, self.send, self.recv = block, send, recv
+    def __init__(self, block, bulk, send, recv, j, m):
+        self.block, self.bulk, self.send, self.recv = block, bulk, send, recv
         self.m, self.lines = m, m // 2
         self.row, self.column = j // 2, lax.rem(j, 2)
         self.facing = j + 1 - 2 * self.column
         self.above_me, self.below_me = lax.rem(j + 2, m), lax.rem(j + m - 2, m)
         self.first, self.last = self.row == 0, self.row == self.lines - 1
 
-    def hop(self, kind, r, device):
-        k = 2 * r + self.column
-        block = self.block(k)
-        return remote(block, block, self.send.at[kind, r], self.recv.at[k], {"tensor": device})
+    def hop(self, send, recv, r, device):
+        block = self.block(2 * r + self.column)
+        return remote(block, block, self.send.at[send], self.recv.at[recv], {"tensor": device})
 
     def up(self, r):
-        return self.hop(0, r, self.above_me)
+        return self.hop(r, r, r, self.above_me)
 
     def down(self, r):
-        return self.hop(1, r, self.below_me)
+        return self.hop(jnp.where(r == self.row, self.lines, r), r, r, self.below_me)
 
     def across(self, r):
-        return self.hop(2, r, self.facing)
+        return self.hop(self.lines + 1, self.lines, r, self.facing)
+
+    def all_across(self):
+        send, recv = self.send.at[self.lines + 1], self.recv.at[self.lines]
+        return remote(self.bulk, self.bulk, send, recv, {"tensor": self.facing})
 
     def sideways(self):
         self.across(self.row).start()
@@ -91,16 +101,11 @@
             self.across(above).start()
 
     def finish(self):
+        self.all_across().wait_recv()
+
+    def drain(self):
+        self.all_across().wait_send()
         for r in range(self.lines):
-            k = 2 * r + 1 - self.column
-            block = self.block(k)
-            remote(
-                block, block, self.send.at[2, r], self.recv.at[k], {"tensor": self.facing}
-            ).wait_recv()
-
-    def drain(self):
-        for r in range(self.lines):
-            self.across(r).wait_send()
             went_up = jnp.logical_and(jnp.logical_not(self.last), r <= self.row)
             went_down = jnp.logical_and(jnp.logical_not(self.first), r >= self.row)
             pl.when(went_up)(lambda: self.up(r).wait_send())
@@ -133,11 +138,11 @@
         mixed_in, x_in, dy_in, gate_in, up_in, down_in,
         out, wg0, wg1, wd,
         dy, x, gate, up, grad_h, down, both, w0, w1, gathered,
-        keep, swap, pair, came, part, beside, carry, rising, falling, mine, final,
+        keep, swap, pair, came, part, beside, carry, rising, mine, final,
         wbuf,
         line_s, line_r, hop_s, hop_r, ge_s, ge_r, gx_s, gx_r, gf_s, gf_r, xs_s, xs_r,
         pair_s, pair_r, ex_s, ex_r, g_s, g_r,
-        y_s, y_r, z_s, up_r, dn_r, load, store, leave,
+        y_s, y_r, z_s, z_r, load, store, leave,
     ):
         me = lax.axis_index("dp")
         j = lax.axis_index("tensor")
@@ -146,8 +151,6 @@
         partner = me + 1 - 2 * core
         z, y = j // 2, lax.rem(j, 2)
         facing = j + 1 - 2 * y
-        above, below = lax.rem(j + 2, m), lax.rem(j + m - 2, m)
-        first, last = z == 0, z == lines - 1
         others = list(range(1, chips))
 
         def shifted(s):
@@ -161,9 +164,9 @@
         for s in range(1, n):
             signal({"dp": lax.rem(me + s, n)})
         signal({"tensor": facing})
-        pl.when(jnp.logical_not(first))(lambda: signal({"tensor": below}))
-        pl.when(jnp.logical_not(last))(lambda: signal({"tensor": above}))
-        pl.semaphore_wait(barrier, n + (z > 0).astype(jnp.int32) + (z < lines - 1).astype(jnp.int32))
+        for d in range(1, lines):
+            signal({"tensor": lax.rem(j + 2 * d, m)})
+        pl.semaphore_wait(barrier, n + lines - 1)
 
         my_half = pl.ds(pl.multiple_of(core * half, half), half)
         its_half = pl.ds(pl.multiple_of((1 - core) * half, half), half)
@@ -226,17 +229,15 @@
             p = 2 * shifted(s) + g
             r = pl.ds(h * half, half)
             return remote(
-                cols_of(x_in, r, p), x.at[me, r], xs_s.at[p, h], xs_r.at[me, h], {"dp": p}
+                cols_of(x_in, r, p), x.at[me, r], xs_s, xs_r.at[me], {"dp": p}
             )
 
         def x_wait():
             near_wait(1, x_in, x)
             for s in others:
                 for g in range(2):
-                    for h in range(2):
-                        q = 2 * shifted(s) + g
-                        spot = x.at[q, pl.ds(h * half, half)]
-                        remote(spot, spot, xs_s.at[q, h], xs_r.at[q, h], {"dp": q}).wait_recv()
+                    q = 2 * shifted(s) + g
+                    remote(x.at[q], x.at[q], xs_s, xs_r.at[q], {"dp": q}).wait_recv()
 
         wide = ((gate_in, gate), (up_in, up))
 
@@ -252,7 +253,7 @@
         def wide_far(a, g, s):
             p = 2 * chip + g
             spot = wide[a][1].at[p, my_half]
-            return remote(spot, spot, gx_s.at[a, g, s], gx_r.at[a, p], {"dp": 2 * shifted(s) + core})
+            return remote(spot, spot, gx_s.at[a, g, s - 1], gx_r.at[a, p], {"dp": 2 * shifted(s) + core})
 
         def wide_forward(a, p):
             spot = wide[a][1].at[p, my_half]
@@ -273,7 +274,14 @@
                     i = base + len(made)
                     q = 2 * shifted(s) + g
                     made.append(
-                        Line(lambda k, q=q: block(buf, q, k), line_s.at[i], line_r.at[i], j, m)
+                        Line(
+                            lambda k, q=q: block(buf, q, k),
+                            buf.at[q, pl.ds(0, half)],
+                            line_s.at[i],
+                            line_r.at[i],
+                            j,
+                            m,
+                        )
                     )
             return made
 
@@ -295,7 +303,7 @@
 
         def ex_copy(p, s):
             q = 2 * shifted(s) + core
-            return remote(swap.at[p], came.at[chip, p], ex_s.at[p, s], ex_r.at[p, chip], {"dp": q})
+            return remote(swap.at[p], came.at[chip, p], ex_s.at[p, s - 1], ex_r.at[p, s - 1], {"dp": q})
 
         def chip_sum(p):
             pair_copy(p).wait()
@@ -322,7 +330,8 @@
             for s in others:
                 q = shifted(s)
                 spot = came.at[q, p]
-                remote(spot, spot, ex_s.at[p, s], ex_r.at[p, q], {"dp": 2 * q + core}).wait_recv()
+                u = chips - s - 1
+                remote(spot, spot, ex_s.at[p, u], ex_r.at[p, u], {"dp": 2 * q + core}).wait_recv()
 
             @pl.loop(0, half // lot)
             def _(i):
@@ -358,75 +367,46 @@
         orders = [sorted(range(lines), key=lambda t: (-abs(t - r), t)) for r in range(lines)]
 
         def target(i):
-            t = jnp.int32(0)
-            for r in range(lines):
-                t = jnp.where(z == r, orders[r][i], t)
-            return t
+            return pick(z, [order[i] for order in orders])
 
         def y_copy(p, i):
             t = target(i)
             src = block(part, p, 2 * t + 1 - y)
-            return remote(src, beside.at[p, t], y_s.at[p, t], y_r.at[p, t], {"tensor": facing})
-
-        def climb(p, t):
-            return remote(carry.at[p, t], rising.at[p, t], z_s.at[p, t], up_r.at[p, t], {"tensor": above})
-
-        def descend(p, t):
-            return remote(carry.at[p, t], falling.at[p, t], z_s.at[p, t], dn_r.at[p, t], {"tensor": below})
-
-        def add_rows(fn):
-            for i in range(rows // lot):
-                fn(slice(i * lot, (i + 1) * lot), i * lot)
+            return remote(src, beside.at[p, t], y_s.at[p], y_r.at[p, t], {"tensor": facing})
+
+        def z_copy(p, t):
+            return remote(
+                carry.at[p, t], rising.at[p, z], z_s.at[p], z_r.at[p], {"tensor": 2 * t + y}
+            )
+
+        def z_all(p):
+            spot = carry.at[p, pl.ds(0, lines - 1)]
+            return remote(spot, spot, z_s.at[p], z_r.at[p], {"tensor": facing})
 
         def item(p, i):
             t = target(i)
             y_copy(p, i).wait_recv()
-            rise = jnp.logical_and(t > z, z > 0)
-            fall = jnp.logical_and(t < z, z < lines - 1)
-            pl.when(rise)(lambda: climb(p, t).wait_recv())
-            pl.when(fall)(lambda: descend(p, t).wait_recv())
-
-            def start_of(r, r0):
-                q = pl.ds(pl.multiple_of((2 * t + y) * rows + r0, lot), lot)
-                return part[p, q].astype(F32) + beside[p, t, r].astype(F32)
-
-            def plain(r, r0):
-                carry[p, t, r] = start_of(r, r0).astype(BF16)
-
-            def risen(r, r0):
-                carry[p, t, r] = (start_of(r, r0) + rising[p, t, r].astype(F32)).astype(BF16)
-
-            def fallen(r, r0):
-                carry[p, t, r] = (start_of(r, r0) + falling[p, t, r].astype(F32)).astype(BF16)
-
-            def own(r, r0):
-                mine[p, r] = start_of(r, r0)
-
-            pl.when(rise)(lambda: add_rows(risen))
-            pl.when(fall)(lambda: add_rows(fallen))
-            edge = jnp.logical_or(jnp.logical_and(first, t > z), jnp.logical_and(last, t < z))
-            pl.when(edge)(lambda: add_rows(plain))
-            pl.when(t == z)(lambda: add_rows(own))
-            pl.when(t > z)(lambda: climb(p, t).start())
-            pl.when(t < z)(lambda: descend(p, t).start())
+            for i0 in range(0, rows, lot):
+                r = slice(i0, i0 + lot)
+                q = pl.ds(pl.multiple_of((2 * t + y) * rows + i0, lot), lot)
+                total = part[p, q].astype(F32) + beside[p, t, r].astype(F32)
+                if i < lines - 1:
+                    carry[p, t, r] = total.astype(BF16)
+                else:
+                    mine[p, r] = total
+            if i < lines - 1:
+                z_copy(p, t).start()
 
         def total_of(p):
-            pl.when(z > 0)(lambda: climb(p, z).wait_recv())
-            pl.when(z < lines - 1)(lambda: descend(p, z).wait_recv())
-
-            def close(parts):
-                def fn(r, r0):
-                    total = mine[p, r]
-                    for ref in parts:
-                        total = total + ref[p, z, r].astype(F32)
-                    final[p, r] = total.astype(BF16)
-
-                return fn
-
-            pl.when(first)(lambda: add_rows(close((falling,))))
-            pl.when(last)(lambda: add_rows(close((rising,))))
-            inner = jnp.logical_not(jnp.logical_or(first, last))
-            pl.when(inner)(lambda: add_rows(close((rising, falling))))
+            sources = [lax.rem(z + d, lines) for d in range(1, lines)]
+            if lines > 1:
+                z_all(p).wait_recv()
+            for i0 in range(0, rows, lot):
+                r = slice(i0, i0 + lot)
+                total = mine[p, r]
+                for q in sources:
+                    total = total + rising[p, q, r].astype(F32)
+                final[p, r] = total.astype(BF16)
 
         def out_copy(p):
             return remote(final.at[p], block(gathered, me, j), hop_s.at[2, p], hop_r.at[2, me], {"dp": p})
@@ -442,7 +422,7 @@
 
         def stored(a, i):
             r = pl.ds(i * tile, tile)
-            return pltpu.make_async_copy(wbuf.at[a, r], grads[a][2].at[r], store.at[a, i])
+            return pltpu.make_async_copy(wbuf.at[a, r], grads[a][2].at[r], store.at[a])
 
         def weights(a, i):
             over_rows = (((0,), (0,)), ((), ()))
@@ -599,31 +579,42 @@
         items(afar(1), "B1", range(1))
         near_chunk(1)
         far_total(0)
+        send_x(0, 1)
         items(afar(1), "B1", range(1, lines))
         items([2 * chip], "A0", range(mid))
         far_total(1)
-        for g, h in ((0, 1), (1, 0), (1, 1)):
-            send_x(g, h)
+        send_x(1, 0)
+        send_x(1, 1)
         items([2 * chip], "A0", range(mid, lines))
         some(1)
-        items([2 * chip + 1], "A1", range(1))
-        with scope("outB0"):
+
+        def open_near():
+            out_wait(partner)
+            out_local().wait()
+            all_of(near_lines, "step", 0)
+
+        def far_arrived():
             for g in range(2):
                 for q in afar(g):
                     out_wait(q)
             all_of(far_lines, "sideways")
-        items([2 * chip + 1], "A1", range(1, lines))
-        all_of(far_lines, "lengthways")
+
+        with scope("farE"):
+            pl.when(core == 0)(far_arrived)
+        items([2 * chip + 1], "A1", every)
+        with scope("farL"):
+            pl.when(core == 1)(far_arrived)
+            all_of(far_lines, "lengthways")
         near_total(0)
+        with scope("nearE"):
+            pl.when(core == 0)(open_near)
         some(1)
         near_total(1)
+        with scope("nearL"):
+            pl.when(core == 1)(open_near)
         if lines > 1:
             with scope("outB1"):
                 all_of(far_lines, "step", 1)
-        with scope("outA0"):
-            out_wait(partner)
-            out_local().wait()
-            all_of(near_lines, "step", 0)
         for d in range(2, lines + 1):
             if d < lines:
                 with scope("outB%d" % d):
@@ -655,9 +646,9 @@
                 for p in afar(g):
                     hop_copy(p).wait_send()
                     out_copy(p).wait_send()
-                for s in others:
-                    for h in range(2):
-                        x_copy(s, g, h).wait_send()
+            if others:
+                spot = x.at[pl.ds(0, n - 2)]
+                remote(spot, spot, xs_s, xs_r.at[me], {"dp": partner}).wait_send()
             near_copy(0, dy_in, dy).wait_send()
             near_copy(1, x_in, x).wait_send()
             out_copy(partner).wait_send()
@@ -668,17 +659,15 @@
                     p = 2 * shifted(s) + g
                     for u in others:
                         ex_copy(p, u).wait_send()
-                    for i in every:
-                        y_copy(p, i).wait_send()
-                        t = target(i)
-                        pl.when(t > z)(lambda: climb(p, t).wait_send())
-                        pl.when(t < z)(lambda: descend(p, t).wait_send())
+                    spot = part.at[p, pl.ds(0, half)]
+                    remote(spot, spot, y_s.at[p], y_r.at[p, 0], {"tensor": facing}).wait_send()
+                    if lines > 1:
+                        z_all(p).wait_send()
         with scope("stores"):
             for q in range(n):
                 leaving(q).wait()
             for a in range(3):
-                for i in range(tiles):
-                    stored(a, i).wait()
+                pltpu.make_async_copy(wbuf.at[a], grads[a][2], store.at[a]).wait()
 
     dma = pltpu.SemaphoreType.DMA
     vm = pltpu.VMEM
@@ -708,35 +697,33 @@
             vm((n, lines, rows, slab), BF16),
             vm((n, lines, rows, slab), BF16),
             vm((n, lines, rows, slab), BF16),
-            vm((n, lines, rows, slab), BF16),
             vm((n, rows, slab), F32),
             vm((n, rows, slab), BF16),
             vm((3, slab, width), BF16),
-            dma((4 * chips - 2, 3, lines)),
-            dma((4 * chips - 2, m)),
+            dma((4 * chips - 2, lines + 2)),
+            dma((4 * chips - 2, lines + 1)),
             dma((3, n)),
             dma((3, n)),
             dma((2,)),
             dma((2,)),
-            dma((2, 2, chips)),
+            dma((2, 2, max(chips - 1, 1))),
             dma((2, n)),
             dma((2, n)),
             dma((2, n)),
-            dma((n, 2)),
-            dma((n, 2)),
-            dma((n,)),
-            dma((n,)),
-            dma((n, chips)),
-            dma((n, chips)),
+            dma,
+            dma((n,)),
+            dma((n,)),
+            dma((n,)),
+            dma((n, max(chips - 1, 1))),
+            dma((n, max(chips - 1, 1))),
+            dma((n,)),
             dma((n,)),
             dma((n,)),
             dma((n, lines)),
-            dma((n, lines)),
-            dma((n, lines)),
-            dma((n, lines)),
-            dma((n, lines)),
+            dma((n,)),
+            dma((n,)),
             dma((5,)),
-            dma((3, tiles)),
+            dma((3,)),
             dma((n,)),
         ],
         cost_estimate=pl.CostEstimate(flops=flops, bytes_accessed=40 * slab * width, transcendentals=0),

time: 118 us -> 114 us (0.966)
  Pallas kernels: 117 us -> 113 us
    pallas_call x1, Pallas kernels: 106 us -> 103 us  [layer(): pl.pallas_call(kernel, out_shape=[jax.ShapeDtypeStruct((n, tokens, slab),...]
where the time goes in v3:
time: 114 us
  Pallas kernels  113 us (99%)
    pallas_call x1, Pallas kernels, layer(): pl.pallas_call(kernel, out_shape=[jax.ShapeDtypeStruct((n, tokens, slab),...  103 us
    pallas_call x1, Pallas kernels, spread_out(): pl.pallas_call(kernel, grid=(steps,), out_shape=[jax.ShapeDtypeStruct((to...  10.5 us

profile of v3, /device:TPU:0, one launch (start us, length us, event | category | flops | bytes accessed | tf_op | source)
XLA Modules:
  0.0 113.7 jit_solution(11163454995201397090)
XLA Ops:
  0.6 102.5 %shard_map.85 = (bf16[4,256,1280]{2,1,0:T(8,128)(2,1)}, bf16[1280,896]{1,0:T(8,128)(2,1)}, bf16[1280,896]{1,0:T(8,128)(2,1)}, bf16[1280,896]{1,0:T(8,128)(2,1)}) custom-call(bf16[1280,2,896]{2,1,0:T(2,128)(2,1)} %refs_0_.1, bf16[256,5120]{1,0:T(8,128)(2,1)} %refs_1_.1, bf16[256,5120]{1,0:T(8,128)(2,1)} %refs_2_.1, bf16[256,896]{1,0:T(8,128)(2,1)} %refs_3_.1, ...), custom_call_target="tpu_custom_call" | custom-call | flops 14092861440 | bytes 45875200 | tf_op jit(solution)/shard_map/pallas_call | solution.py:675
  103.2 10.5 %shard_map.86 = (bf16[256,5120]{1,0:T(8,128)(2,1)}, f32[1280,2,896]{2,1,0:T(2,128)}, f32[1280,896]{1,0:T(8,128)}) custom-call(bf16[4,256,1280]{2,1,0:T(8,128)(2,1)} %get-tuple-element.7.all_ref, bf16[1280,896]{1,0:T(8,128)(2,1)} %get-tuple-element.8.gate_ref, bf16[1280,896]{1,0:T(8,128)(2,1)} %get-tuple-element.9.up_ref, ...), custom_call_target="tpu_custom_call" | custom-call | flops 1146880 | bytes 20643840 | tf_op jit(solution)/shard_map/pallas_call | solution.py:750
